TPU v7x, 32 devices: a whole 2x2x4 slice. The times are simulated.
32 devices in a mesh: dp: 8 (over z, core), fsdp: 4 (over y, x).
Axes of the slice: x: 2, y: 2, z: 4, core: 2. Of those that a mesh axis runs over, the one named last changes fastest.
Arguments:
- logits: bfloat16 [4096, 32000], P('dp', 'fsdp'), may hold values from -115 to 125
- labels: int32 [4096], P('dp'), may hold values from 0 to 31999
- activations: bfloat16 [4096, 5120], P('dp', 'fsdp'), may hold values from -6 to 6
- proj_in: bfloat16 [5120, 64], P('fsdp'), may hold values from -0.078125 to 0.078125
- proj_out: bfloat16 [32000, 64], P('fsdp'), may hold values from -6 to 6
Outputs:
- features: float32 [512, 4096], P(('dp', 'fsdp'))
- gram: float32 [4096, 4096], P('fsdp', 'dp')
All inputs are finite; a program needn't handle non-finite values.
Results may differ from a plain program's by a relative error of at most 0.014.
Values may be sent and summed in bfloat16 or wider, within the bound.
No kernel may reach another device: no remote copies, remote signals or barrier semaphores. Data moves between devices by JAX's collectives and lax.ppermute only.
A program may use at most 64 MiB of HBM per device.

v0:
```python
import jax
import jax.numpy as jnp
from jax import lax
from jax.sharding import PartitionSpec as P

SEQ = 8


def body(logits, labels, activations, proj_in, proj_out):
    vocab_local = logits.shape[1]
    values = logits.astype(jnp.float32)
    local_top = jnp.max(values, axis=1)
    row_top = lax.pmax(local_top, "fsdp")
    row_sum = lax.psum(jnp.sum(jnp.exp(values - row_top[:, None]), axis=1), "fsdp")
    prob = jnp.exp(values - row_top[:, None]) / row_sum[:, None]
    columns = lax.axis_index("fsdp") * vocab_local + lax.broadcasted_iota(
        jnp.int32, (1, vocab_local), 1
    )
    onehot = (columns == labels[:, None]).astype(jnp.float32)
    errors = (prob - onehot).astype(jnp.bfloat16)
    part_left = jnp.dot(activations, proj_in, preferred_element_type=jnp.float32)
    part_right = jnp.dot(errors, proj_out, preferred_element_type=jnp.float32)
    left, right = (
        lax.psum_scatter(part_left, "fsdp", scatter_dimension=0, tiled=True),
        lax.psum_scatter(part_right, "fsdp", scatter_dimension=0, tiled=True),
    )
    count = left.shape[0] // SEQ
    width_in = proj_in.shape[1]
    width_out = proj_out.shape[1]
    sketch = jnp.einsum(
        "esi,esj->eij", left.reshape(count, SEQ, width_in), right.reshape(count, SEQ, width_out)
    )
    features = sketch.reshape(count, width_in * width_out)
    rounded = features.astype(jnp.bfloat16)
    feat_all = features.shape[1]
    gram_rows = feat_all // lax.axis_size("fsdp")
    row_start = lax.axis_index("fsdp") * gram_rows
    folded = lax.all_gather(rounded, "fsdp", axis=0, tiled=True)
    column_share = lax.all_to_all(folded, "dp", split_axis=1, concat_axis=0, tiled=True)
    row_share = lax.dynamic_slice_in_dim(folded, row_start, gram_rows, 1)
    gram = lax.dot_general(
        lax.all_gather(row_share, "dp", axis=0, tiled=True),
        column_share,
        (((0,), (0,)), ((), ())),
        preferred_element_type=jnp.float32,
    )
    return (features, gram)


def solution(mesh):
    in_specs = (P("dp", "fsdp"), P("dp"), P("dp", "fsdp"), P("fsdp", None), P("fsdp", None))
    out_specs = (P(("dp", "fsdp"), None), P("fsdp", "dp"))
    return jax.shard_map(body, mesh=mesh, in_specs=in_specs, out_specs=out_specs, check_vma=False)
```

profile of v0, /device:TPU:0, one launch (start us, length us, event | category | flops | bytes accessed | tf_op | source)
XLA Modules:
  0.0 152.0 jit_solution(3357230668672112707)
XLA Ops:
  7.2 0.0 copy-start
  7.2 0.0 reduce-scatter.5.cloned.1.call-start
  7.2 4.6 %reduce_max.14 = bf16[512]{0:T(512)(128)(2,1)S(1)} reduce(bf16[512,8000]{0,1:T(8,128)(2,1)} %param.5, bf16[]{:T(256)} %constant.7.clone.1), dimensions={1}, to_apply=%region_1.0 | reduce | flops 4095488 | bytes 8193026 | tf_op jit(solution)/shard_map/reduce_max | solution.py:12
  11.9 11.4 %pmax.7 = f32[512]{0:T(512)S(1)} all-reduce(bf16[512]{0:T(512)(128)(2,1)S(1)} %reduce_max.14), channel_id=1, replica_groups=mesh['dp'=8,'fsdp'=4] {'fsdp'}, use_global_device_ids=true, to_apply=%region_2.0 | all-reduce | flops 512 | bytes 3072 | tf_op jit(solution)/shard_map/pmax | solution.py:13
  23.2 6.1 %fusion = f32[512]{0:T(512)S(1)} fusion(bf16[512,8000]{0,1:T(8,128)(2,1)} %param.5, f32[512]{0:T(512)S(1)} %pmax.7), kind=kLoop, calls=%fused_computation.2 | loop fusion | flops 12287488 | bytes 8196096 | tf_op jit(solution)/shard_map/reduce_sum | solution.py:14
  29.3 8.0 %psum.7 = f32[512]{0:T(512)S(1)} all-reduce(f32[512]{0:T(512)S(1)} %fusion), channel_id=1, replica_groups=mesh['dp'=8,'fsdp'=4] {'fsdp'}, use_global_device_ids=true, to_apply=%region_4.0 | all-reduce | flops 512 | bytes 4096 | tf_op jit(solution)/shard_map/psum | solution.py:14
  37.3 10.7 %fusion.1 = f32[512,64]{0,1:T(8,128)} fusion(bf16[8000,64]{0,1:T(8,128)(2,1)S(1)} %copy-done.3, bf16[512,8000]{0,1:T(8,128)(2,1)} %param.5, s32[512]{0:T(512)S(1)} %copy-done.4, f32[512]{0:T(512)S(1)} %psum.7, f32[512]{0:T(512)S(1)} %pmax.7, s32[8000]{0:T(1024)S(1)} %iota_add_fusion), kind=kOutput, calls=%fused_computation.3 | convolution fusion | flops 552960000 | bytes 9385216 | tf_op jit(solution)/shard_map/dot_general | solution.py:22
  48.0 0.0 reduce-scatter.5.cloned.1.call-update
  48.0 0.0 reduce-scatter.3.cloned.1.call-start
  48.1 1.2 fusion.5
  49.3 0.0 reduce-scatter.3.cloned.1.call-update
  49.3 0.0 all-gather.2.cloned.1.call-start
  49.3 23.3 %reduce-scatter.5.cloned.1.call-done = f32[128,64]{0,1:T(8,128)} async-done(((f32[512,64]{0,1:T(8,128)}), f32[128,64]{0,1:T(8,128)}) %reduce-scatter.5.cloned.1.call-update) | async-done | bytes 32784 | tf_op jit(solution)/shard_map/reduce_scatter | solution.py:25
  72.6 0.9 copy.15
  73.5 26.6 %reduce-scatter.3.cloned.1.call-done = f32[128,64]{0,1:T(8,128)} async-done(((f32[512,64]{0,1:T(8,128)}), f32[128,64]{0,1:T(8,128)}) %reduce-scatter.3.cloned.1.call-update) | async-done | bytes 32784 | tf_op jit(solution)/shard_map/reduce_scatter | solution.py:24
  100.1 0.9 copy.14
  101.0 0.3 fusion.2
  101.3 0.2 reshape.26
  101.5 10.5 %all_gather.6 = bf16[64,4096]{1,0:T(8,128)(2,1)S(1)} all-gather(bf16[16,4096]{1,0:T(8,128)(2,1)S(1)} %convert_element_type.15), channel_id=1, replica_groups=mesh['dp'=8,'fsdp'=4] {'fsdp'}, dimensions={0}, use_global_device_ids=true | all-gather | bytes 655360 | tf_op jit(solution)/shard_map/all_gather | solution.py:38
  112.0 0.7 constant_dynamic-slice_fusion
  112.6 0.0 all-gather.2.cloned.1.call-update
  112.7 28.1 %all_to_all.19 = bf16[64,8,512]{2,0,1:T(8,128)(2,1)S(1)} all-to-all(bf16[64,8,512]{2,0,1:T(8,128)(2,1)S(1)} %bitcast.20), channel_id=1, replica_groups=mesh['dp'=8,'fsdp'=4] {'dp'}, dimensions={1} | all-to-all | bytes 1048576 | tf_op jit(solution)/shard_map/all_to_all | solution.py:39
  140.9 1.4 all-gather.2.cloned.1.call-done
  142.2 3.3 %fusion.6 = f32[1024,512]{1,0:T(8,128)} fusion(bf16[512,1024]{1,0:T(8,128)(2,1)} %all-gather.2.cloned.1.call-done, bf16[512,512]{1,0:T(8,128)(2,1)S(1)} %bitcast.19), kind=kOutput, calls=%fused_computation.11 | convolution fusion | flops 536870912 | bytes 3670016 | tf_op jit(solution)/shard_map/dot_general | solution.py:41
  (12 shorter events, 0.1 us)
Async XLA Ops:
  7.2 40.9 %copy-start = (bf16[512,1280]{1,0:T(8,128)(2,1)S(1)}, bf16[512,1280]{1,0:T(8,128)(2,1)}, u32[]{:S(2)}) copy-start(bf16[512,1280]{1,0:T(8,128)(2,1)} %param.7) | copy-start | bytes 3932164
  7.2 65.4 %reduce-scatter.5.cloned.1.call-start = ((), (), s32[]{:S(2)}) async-start(), calls=%async_computation.4 | async-start | bytes 163840 | tf_op jit(solution)/shard_map/reduce_scatter | solution.py:25
  7.2 30.1 %copy-start.3 = (bf16[8000,64]{0,1:T(8,128)(2,1)S(1)}, bf16[8000,64]{0,1:T(8,128)(2,1)}, u32[]{:S(2)}) copy-start(bf16[8000,64]{0,1:T(8,128)(2,1)} %param.9) | copy-start | bytes 3072004
  7.2 30.1 %copy-start.4 = (s32[512]{0:T(512)S(1)}, s32[512]{0:T(512)}, u32[]{:S(2)}) copy-start(s32[512]{0:T(512)} %param.6) | copy-start | bytes 6148
  37.3 10.8 %copy-start.2 = (bf16[1280,64]{0,1:T(8,128)(2,1)S(1)}, bf16[1280,64]{0,1:T(8,128)(2,1)}, u32[]{:S(2)}) copy-start(bf16[1280,64]{0,1:T(8,128)(2,1)} %param.8) | copy-start | bytes 491524
  48.0 52.1 %reduce-scatter.3.cloned.1.call-start = ((), (), s32[]{:S(2)}) async-start(), calls=%async_computation.3 | async-start | bytes 163840 | tf_op jit(solution)/shard_map/reduce_scatter | solution.py:24
  49.3 92.9 %all-gather.2.cloned.1.call-start = ((), (), s32[]{:S(2)}) async-start(), calls=%async_computation.5 | async-start | bytes 1179648 | tf_op jit(solution)/shard_map/all_gather | solution.py:42
  101.5 44.0 %copy-start.1 = (f32[16,4096]{1,0:T(8,128)}, f32[16,4096]{1,0:T(8,128)S(1)}, u32[]{:S(2)}) copy-start(f32[16,4096]{1,0:T(8,128)S(1)} %reshape.26) | copy-start | bytes 786436
Sparse Core Ops, SparseCore 0:
  48.1 24.4 reduce-scatter.4
  75.9 24.1 reduce-scatter.2
  112.8 29.3 all-gather.1
where the time goes:
time: 153 us; the launch traced here: 152 us
  blocking collectives  58 us (38%)
  waiting for transfers between devices  51.3 us (34%)
  matrix products  15.4 us (10%)
  between operations  13.8 us (9%)
  other arithmetic  10.7 us (7%)
  local copies, waits for them, and re-layouts  2.64 us (2%)
    all_to_all x1, blocking collectives, body(): lax.all_to_all(folded, 'dp', split_axis=1, concat_axis=0, tiled=True)  28.1 us
    reduce_scatter x1, waiting for transfers between devices, body(): lax.psum_scatter(part_left, 'fsdp', scatter_dimension=0, tiled=True)  26.6 us
    reduce_scatter x1, waiting for transfers between devices, body(): lax.psum_scatter(part_right, 'fsdp', scatter_dimension=0, tiled=True)  23.3 us
    pmax x1, blocking collectives, body(): row_top = lax.pmax(local_top, 'fsdp')  11.4 us
    dot_general x1, matrix products, body(): part_right = jnp.dot(errors, proj_out, preferred_element_type=jnp.float32)  10.7 us
    all_gather x1, blocking collectives, body(): folded = lax.all_gather(rounded, 'fsdp', axis=0, tiled=True)  10.5 us
    psum x1, blocking collectives, body(): lax.psum(jnp.sum(jnp.exp(values - row_top[:, None]), axis=1), 'fsdp')  7.98 us
    reduce_sum x1, other arithmetic, body(): jnp.sum(jnp.exp(values - row_top[:, None]), axis=1)  6.09 us
  transfers between devices with their start and end apart: 3, of which 3 were waited for; matrix products, arithmetic and copies ran while one was open for 1% of the time, Pallas kernels for 0%

commit v1 on v0

v1 whole, which is shorter than its diff:
```python
import functools

import jax
import jax.numpy as jnp
from jax import lax
from jax.experimental import pallas as pl
from jax.experimental.pallas import tpu as pltpu
from jax.sharding import PartitionSpec as P

SEQ = 8
LOG2E = 1.4426950408889634
LANES = 128
CHUNK = 1024
SUB = 256
STAT = 16
F32 = jnp.float32
BF16 = jnp.bfloat16


def _cdiv(a, b):
    return (a + b - 1) // b


def _sizes(total, step):
    out = []
    start = 0
    while start < total:
        out.append((start, min(step, total - start)))
        start += step
    return out


def _local_kernel(
    logits_hbm, labels_hbm, act_hbm, pin_hbm, pout_hbm, *rest, groups, vocab, tokens, width, k_in, k_out
):
    outs = rest[:groups]
    buf, lab, act, pin, pext, acc, plab, top, msg, sem, lsem = rest[groups:]
    copies = [
        pltpu.make_async_copy(pin_hbm, pin, sem.at[0]),
        pltpu.make_async_copy(act_hbm, act, sem.at[1]),
        pltpu.make_async_copy(pout_hbm, pext.at[0:k_out, :], sem.at[2]),
        pltpu.make_async_copy(labels_hbm, lab, sem.at[3]),
    ]
    for c in copies:
        c.start()
    chunks = _sizes(vocab, CHUNK)
    loads = []
    for n, (start, size) in enumerate(chunks):
        c = pltpu.make_async_copy(logits_hbm.at[start : start + size, :], buf.at[start : start + size, :], lsem.at[n])
        c.start()
        loads.append(c)
    mine = lax.axis_index("fsdp")
    copies[0].wait()
    copies[1].wait()
    left = lax.dot_general(pin[...], act[...], (((1,), (1,)), ((), ())), preferred_element_type=F32)
    msg[0:k_in, :] = left.astype(BF16)
    copies[2].wait()
    copies[3].wait()
    pext[k_out : k_out + STAT, :] = jnp.ones((STAT, vocab), BF16)
    acc[...] = jnp.zeros_like(acc)
    plab[...] = jnp.zeros_like(plab)
    top[...] = jnp.full_like(top, -1e30)
    local = lab[...] - mine * vocab
    inside = (local >= 0) & (local < vocab)
    local = jnp.where(inside, local, -LANES)
    block = lax.shift_right_arithmetic(local, 7)
    lane = jnp.bitwise_and(local, LANES - 1)

    for n, (start, size) in enumerate(chunks):
        loads[n].wait()
        peak = None
        for r, h in _sizes(size, 16):
            part = buf[start + r : start + r + h, :]
            peak = part if peak is None else jnp.maximum(peak, part)
        peak = jnp.max(peak.astype(F32), axis=0, keepdims=True)
        old = top[...]
        new = jnp.maximum(old, peak)
        top[...] = new
        keep = jnp.exp2((old - new) * LOG2E)
        total = acc[...] * keep
        for r, h in _sizes(size, SUB):
            part = buf[start + r : start + r + h, :].astype(F32)
            expo = jnp.exp2((part - new) * LOG2E).astype(BF16)
            total = total + jnp.dot(pext[:, start + r : start + r + h], expo, preferred_element_type=F32)
        acc[...] = total
        for t in range(_cdiv(tokens, LANES)):
            cols = slice(t * LANES, (t + 1) * LANES)
            which = jnp.broadcast_to(block[:, cols], (k_out, LANES))
            index = jnp.broadcast_to(lane[:, cols], (k_out, LANES))
            found = plab[:, cols]
            for r, h in _sizes(size, LANES):
                tile = pext[0:k_out, start + r : start + r + h].astype(F32)
                if h < LANES:
                    tile = jnp.concatenate([tile, jnp.zeros((k_out, LANES - h), F32)], axis=1)
                got = jnp.take_along_axis(tile, index, axis=1)
                found = jnp.where(which == (start + r) // LANES, got, found)
            plab[:, cols] = found

    msg[k_in : k_in + k_out, :] = acc[0:k_out, :].astype(BF16)
    msg[k_in + k_out : k_in + 2 * k_out, :] = plab[...].astype(BF16)
    sums = acc[k_out : k_out + STAT, :]
    high = sums.astype(BF16).astype(F32)
    row = lax.broadcasted_iota(jnp.int32, (STAT, tokens), 0)
    stat = jnp.where(row == 0, top[...], jnp.where(row == 1, high, jnp.where(row == 2, sums - high, 0.0)))
    msg[k_in + 2 * k_out :, :] = stat.astype(BF16)
    share = tokens // groups
    examples = tokens // SEQ
    src = lax.broadcasted_iota(jnp.int32, (tokens, tokens), 0)
    dst = lax.broadcasted_iota(jnp.int32, (tokens, tokens), 1) + mine * share
    dst = jnp.where(dst >= tokens, dst - tokens, dst)
    want = jnp.bitwise_and(dst, examples - 1) * SEQ + lax.shift_right_arithmetic(dst, examples.bit_length() - 1)
    moved = jnp.dot(msg[...], jnp.where(src == want, 1.0, 0.0).astype(BF16), preferred_element_type=F32).astype(BF16)
    for k in range(groups):
        outs[k][...] = moved[:, k * share : (k + 1) * share]


def _local(logits, labels, act, pin, pout, groups):
    vocab, tokens = logits.shape
    k_in, width = pin.shape
    k_out = pout.shape[0]
    rows = k_in + 2 * k_out + STAT
    share = tokens // groups
    n_chunks = _cdiv(vocab, CHUNK)
    any_spec = pl.BlockSpec(memory_space=pl.ANY)
    return pl.pallas_call(
        functools.partial(
            _local_kernel, groups=groups, vocab=vocab, tokens=tokens, width=width, k_in=k_in, k_out=k_out
        ),
        out_shape=[jax.ShapeDtypeStruct((rows, share), BF16)] * groups,
        in_specs=[any_spec] * 5,
        out_specs=[pl.BlockSpec(memory_space=pltpu.VMEM)] * groups,
        scratch_shapes=[
            pltpu.VMEM((vocab, tokens), BF16),
            pltpu.VMEM((1, tokens), jnp.int32),
            pltpu.VMEM((tokens, width), BF16),
            pltpu.VMEM((k_in, width), BF16),
            pltpu.VMEM((k_out + STAT, vocab), BF16),
            pltpu.VMEM((k_out + STAT, tokens), F32),
            pltpu.VMEM((k_out, tokens), F32),
            pltpu.VMEM((1, tokens), F32),
            pltpu.VMEM((rows, tokens), BF16),
            pltpu.SemaphoreType.DMA((4,)),
            pltpu.SemaphoreType.DMA((n_chunks,)),
        ],
        name="local_pass",
    )(logits, labels, act, pin, pout)


def _join_kernel(*refs, k_in, k_out):
    parts, out = refs[:-1], refs[-1]
    base = k_in + 2 * k_out
    stats = [p[base : base + STAT, :].astype(F32) for p in parts]
    top = functools.reduce(jnp.maximum, [s[0:1] for s in stats])
    weights = [jnp.exp2((s[0:1] - top) * LOG2E) for s in stats]
    total = sum(w * (s[1:2] + s[2:3]) for w, s in zip(weights, stats))
    scale = 1.0 / total
    left = sum(p[0:k_in, :].astype(F32) for p in parts)
    right = sum(p[k_in : k_in + k_out, :].astype(F32) * w for p, w in zip(parts, weights)) * scale
    right = right - sum(p[k_in + k_out : base, :].astype(F32) for p in parts)
    out[0:k_in, :] = left.astype(BF16)
    out[k_in : k_in + k_out, :] = right.astype(BF16)


def _join(parts, k_in, k_out):
    return pl.pallas_call(
        functools.partial(_join_kernel, k_in=k_in, k_out=k_out),
        out_shape=jax.ShapeDtypeStruct((k_in + k_out, parts[0].shape[1]), BF16),
        in_specs=[pl.BlockSpec(memory_space=pltpu.VMEM)] * len(parts),
        out_specs=pl.BlockSpec(memory_space=pltpu.VMEM),
        name="join",
    )(*parts)


def _gram_body(x, out_hbm, frow, fcol, res, sem, n_row, n_col, k_out):
    lanes = x.shape[2]
    base = n_row + n_col

    def feature_rows(first, count, dest, dest_first):
        for z in range(lanes // LANES):
            cols = slice(z * LANES, (z + 1) * LANES)
            for j in range(0, k_out, 16):
                rights = [x[t, base + j : base + j + 16, cols] for t in range(SEQ)]
                for i in range(count):
                    total = None
                    for t in range(SEQ):
                        term = x[t, first + i : first + i + 1, cols] * rights[t]
                        total = term if total is None else total + term
                    at = dest_first + i * k_out + j
                    dest[at : at + 16, cols] = total.astype(BF16)

    feature_rows(n_row, n_col, fcol, 0)
    step = max(1, n_row // 4)
    copies = []
    for b, i in enumerate(range(0, n_row, step)):
        feature_rows(i, step, frow, i * k_out)
        rows = slice(i * k_out, (i + step) * k_out)
        res[rows, :] = lax.dot_general(
            frow[rows, :], fcol[...], (((1,), (1,)), ((), ())), preferred_element_type=F32
        )
        c = pltpu.make_async_copy(res.at[rows, :], out_hbm.at[rows, :], sem.at[b])
        c.start()
        copies.append(c)
    for c in copies:
        c.wait()


def _gram_kernel(*refs, n_in, blocks, examples, n_row, n_col, k_in, k_out):
    ins, out_hbm = refs[:n_in], refs[n_in]
    x, frow, fcol, res, sem = refs[n_in + 1 :]
    rows = k_in + k_out
    half = n_in // 2
    if blocks:
        row_first = lax.axis_index("fsdp") * n_row
        col_first = lax.axis_index("dp") * n_col
        per = LANES // examples
        for k in range(half):
            for z in range(blocks):
                takes = [
                    (pl.ds(pl.multiple_of(z * rows + row_first, 8), n_row), 0, n_row),
                    (pl.ds(pl.multiple_of(z * rows + col_first, 8), n_col), n_row, n_col),
                    (slice(z * rows + k_in, (z + 1) * rows), n_row + n_col, k_out),
                ]
                for take, at, count in takes:
                    own = ins[k][take, :].astype(F32)
                    other = ins[half + k][take, :].astype(F32)
                    for s in range(per):
                        piece = slice(s * examples, (s + 1) * examples)
                        x[k * per + s, at : at + count, z * LANES : (z + 1) * LANES] = jnp.concatenate(
                            [own[:, piece], other[:, piece]], axis=1
                        )
    else:
        x[...] = ins[0][...].astype(F32)
    _gram_body(x, out_hbm, frow, fcol, res, sem, n_row, n_col, k_out)


def _gram(ins, blocks, examples, lanes, n_row, n_col, k_in, k_out):
    rows, cols = n_row * k_out, n_col * k_out
    return pl.pallas_call(
        functools.partial(
            _gram_kernel,
            n_in=len(ins),
            blocks=blocks,
            examples=examples,
            n_row=n_row,
            n_col=n_col,
            k_in=k_in,
            k_out=k_out,
        ),
        out_shape=jax.ShapeDtypeStruct((rows, cols), F32),
        in_specs=[pl.BlockSpec(memory_space=pltpu.VMEM)] * len(ins),
        out_specs=pl.BlockSpec(memory_space=pl.ANY),
        scratch_shapes=[
            pltpu.VMEM((SEQ, n_row + n_col + k_out, lanes), F32),
            pltpu.VMEM((rows, lanes), BF16),
            pltpu.VMEM((cols, lanes), BF16),
            pltpu.VMEM((rows, cols), F32),
            pltpu.SemaphoreType.DMA((8,)),
        ],
        name="gram",
    )(*ins)


def body(logits, labels, activations, proj_in, proj_out):
    n_f, n_d = lax.axis_size("fsdp"), lax.axis_size("dp")
    tokens = logits.shape[0]
    k_in, k_out = proj_in.shape[1], proj_out.shape[1]
    rows = k_in + k_out
    examples = tokens // SEQ
    own_examples = examples // n_f
    share = tokens // n_f

    def along_f(a, k):
        return lax.ppermute(a, "fsdp", [(i, (i + k) % n_f) for i in range(n_f)])

    def along_z(a, k):
        return lax.ppermute(a, "dp", [(i, (i + 2 * k) % n_d) for i in range(n_d)])

    def other_core(a):
        return lax.ppermute(a, "dp", [(i, i ^ 1) for i in range(n_d)])

    parts = _local(logits.T, labels.reshape(1, tokens), activations, proj_in.T, proj_out.T, n_f)
    parts = [parts[0]] + [along_f(parts[k], k) for k in range(1, n_f)]
    joined = _join(parts, k_in, k_out)
    n_z = n_d // 2
    column = jnp.concatenate([joined] + [along_z(joined, k) for k in range(1, n_z)], axis=0)
    own = [column] + [along_f(column, k) for k in range(1, n_f)]
    other = [other_core(a) for a in own]

    mine = lax.axis_index("fsdp")
    if share >= examples:
        slots = share // examples
        pieces = []
        for a in own:
            part = a[:rows].reshape(rows, slots, examples)
            pieces.append(lax.dynamic_slice_in_dim(part, mine * own_examples, own_examples, 2))
        group = jnp.concatenate(pieces, axis=1)
    else:
        order = [(mine - k) % n_f for k in range(n_f)]
        whole = jnp.zeros((n_f, rows, share), BF16)
        for k, a in enumerate(own):
            whole = lax.dynamic_update_slice(whole, a[:rows][None], (order[k], 0, 0))
        whole = whole.transpose(1, 0, 2).reshape(rows, SEQ, examples)
        group = lax.dynamic_slice_in_dim(whole, mine * own_examples, own_examples, 2)
    features = jnp.einsum("ite,jte->eij", group[:k_in], group[k_in:], preferred_element_type=F32)
    features = features.reshape(own_examples, k_in * k_out)

    n_row, n_col = k_in // n_f, k_in // n_d
    lanes = examples * n_d
    if share == LANES and 2 * examples == LANES and n_row % 8 == 0 and n_col % 8 == 0:
        gram = _gram(own + other, n_z, examples, lanes, n_row, n_col, k_in, k_out)
    else:
        order = [(mine - k) % n_f for k in range(n_f)]
        whole = jnp.zeros((n_f, 2, n_z, rows, share), BF16)
        for c, arrays in enumerate((own, other)):
            for k, a in enumerate(arrays):
                whole = lax.dynamic_update_slice(whole, a.reshape(1, 1, n_z, rows, share), (order[k], c, 0, 0, 0))
        whole = whole.transpose(3, 1, 2, 0, 4).reshape(rows, 2, n_z, SEQ, examples)
        whole = whole.transpose(3, 0, 1, 2, 4).reshape(SEQ, rows, lanes)
        whole = jnp.concatenate(
            [
                lax.dynamic_slice_in_dim(whole, mine * n_row, n_row, 1),
                lax.dynamic_slice_in_dim(whole, lax.axis_index("dp") * n_col, n_col, 1),
                whole[:, k_in:],
            ],
            axis=1,
        )
        gram = _gram([whole], 0, examples, lanes, n_row, n_col, k_in, k_out)
    return features, gram


def solution(mesh):
    in_specs = (P("dp", "fsdp"), P("dp"), P("dp", "fsdp"), P("fsdp", None), P("fsdp", None))
    out_specs = (P(("dp", "fsdp"), None), P("fsdp", "dp"))
    return jax.shard_map(body, mesh=mesh, in_specs=in_specs, out_specs=out_specs, check_vma=False)
```

time: 153 us -> 47.4 us (0.31)
  blocking collectives: 58 us -> 0 us
  waiting for transfers between devices: 51.3 us -> 8.9 us
  Pallas kernels: 0 us -> 16.4 us
  starting transfers between devices: 0.12 us -> 15.7 us
  matrix products: 15.4 us -> 0.3 us
  between operations: 13.8 us -> 0.81 us
  other arithmetic: 10.7 us -> 0.81 us
    reduce_scatter x2 -> x0, waiting for transfers between devices: 49.9 us -> none  [the longest x1 26.6 us: body(): lax.psum_scatter(part_left, 'fsdp', scatter_dimension=0, tiled=True)]
    all_to_all x1 -> x0, blocking collectives: 28.1 us -> none  [body(): lax.all_to_all(folded, 'dp', split_axis=1, concat_axis=0, tiled=True)]
    pallas_call x0 -> x3, Pallas kernels: none -> 16.4 us  [the longest x1 9.41 us: _local(): pl.pallas_call(functools.partial(_local_kernel, groups=groups, vocab=voca...]
    ppermute x0 -> x13, starting transfers between devices: none -> 15.7 us  [the longest x6 9.46 us: along_f(): return lax.ppermute(a, 'fsdp', [(i, (i + k) % n_f) for i in range(n_f)])]
    dot_general x4 -> x1, matrix products: 15.4 us -> 0.3 us  [body(): jnp.einsum('ite,jte->eij', group[:k_in], group[k_in:], preferred_element_...]
    pmax x1 -> x0, blocking collectives: 11.4 us -> none  [body(): row_top = lax.pmax(local_top, 'fsdp')]
    all_gather x1 -> x0, blocking collectives: 10.5 us -> none  [body(): folded = lax.all_gather(rounded, 'fsdp', axis=0, tiled=True)]
    ppermute x0 -> x13, waiting for transfers between devices: none -> 8.9 us  [the longest x6 6.09 us: along_f(): return lax.ppermute(a, 'fsdp', [(i, (i + k) % n_f) for i in range(n_f)])]
  transfers between devices with their start and end apart: 3 -> 13, of which waited for: 3 -> 9; matrix products, arithmetic and copies ran while one was open for 1% -> 5% of each run, Pallas kernels for 0% -> 0%
where the time goes in v1:
time: 47.4 us; the launch traced here: 47 us
  Pallas kernels  16.4 us (35%)
  starting transfers between devices  15.7 us (33%)
  waiting for transfers between devices  8.9 us (19%)
  local copies, waits for them, and re-layouts  4.12 us (9%)
  other arithmetic  0.81 us (2%)
  between operations  0.81 us (2%)
    ppermute x6, starting transfers between devices, along_f(): return lax.ppermute(a, 'fsdp', [(i, (i + k) % n_f) for i in range(n_f)])  9.46 us
    pallas_call x1, Pallas kernels, _local(): pl.pallas_call(functools.partial(_local_kernel, groups=groups, vocab=voca...  9.41 us
    ppermute x6, waiting for transfers between devices, along_f(): return lax.ppermute(a, 'fsdp', [(i, (i + k) % n_f) for i in range(n_f)])  6.09 us
    ppermute x3, starting transfers between devices, along_z(): return lax.ppermute(a, 'dp', [(i, (i + 2 * k) % n_d) for i in range(n_d)])  5.52 us
    pallas_call x1, Pallas kernels, _gram(): pl.pallas_call(functools.partial(_gram_kernel, n_in=len(ins), blocks=bloc...  5.45 us
    ppermute x3, waiting for transfers between devices, along_z(): return lax.ppermute(a, 'dp', [(i, (i + 2 * k) % n_d) for i in range(n_d)])  2.77 us
    unnamed x26, local copies, waits for them, and re-layouts  2 us
    pallas_call x1, Pallas kernels, _join(): pl.pallas_call(functools.partial(_join_kernel, k_in=k_in, k_out=k_out), o...  1.54 us
  transfers between devices with their start and end apart: 13, of which 9 were waited for; matrix products, arithmetic and copies ran while one was open for 5% of the time, Pallas kernels for 0%

profile of v1, /device:TPU:0, one launch (start us, length us, event | category | flops | bytes accessed | tf_op | source)
XLA Modules:
  0.0 47.0 jit_solution(12913635979842842540)
XLA Ops:
  0.6 9.4 %local_pass.1 = (bf16[208,128]{1,0:T(8,128)(2,1)}, bf16[208,128]{1,0:T(8,128)(2,1)}, bf16[208,128]{1,0:T(8,128)(2,1)}, bf16[208,128]{1,0:T(8,128)(2,1)}) custom-call(bf16[8000,512]{1,0:T(8,128)(2,1)} %bitcast.8, s32[1,512]{1,0:T(1,128)} %bitcast.15, bf16[512,1280]{1,0:T(8,128)(2,1)} %act_hbm.1, bf16[64,1280]{1,0:T(8,128)(2,1)} %bitcast.10, ...), custom_call_target="tpu_custom_call" | custom-call | tf_op jit(solution)/shard_map/local_pass/pallas_call | solution.py:125
  10.1 3.0 %collective-permute-start = (bf16[208,128]{1,0:T(8,128)(2,1)}, bf16[208,128]{1,0:T(8,128)(2,1)S(1)}, u32[]{:S(2)}, u32[]{:S(2)}) collective-permute-start(bf16[208,128]{1,0:T(8,128)(2,1)} %get-tuple-element.7), channel_id=1, source_target_pairs={{0,1},{1,2},{2,3},{3,0},{4,5},{5,6},{6,7},{7,4},{8,9},{9,10},{10,1... | collective-permute-start | bytes 159752 | tf_op jit(solution)/shard_map/ppermute | solution.py:273
  13.1 1.5 %collective-permute-start.1 = (bf16[208,128]{1,0:T(8,128)(2,1)}, bf16[208,128]{1,0:T(8,128)(2,1)S(1)}, u32[]{:S(2)}, u32[]{:S(2)}) collective-permute-start(bf16[208,128]{1,0:T(8,128)(2,1)} %get-tuple-element.8), channel_id=1, source_target_pairs={{0,2},{1,3},{2,0},{3,1},{4,6},{5,7},{6,4},{7,5},{8,10},{9,11},{10,... | collective-permute-start | bytes 159752 | tf_op jit(solution)/shard_map/ppermute | solution.py:273
  14.6 1.4 %collective-permute-start.2 = (bf16[208,128]{1,0:T(8,128)(2,1)}, bf16[208,128]{1,0:T(8,128)(2,1)S(1)}, u32[]{:S(2)}, u32[]{:S(2)}) collective-permute-start(bf16[208,128]{1,0:T(8,128)(2,1)} %get-tuple-element.9), channel_id=1, source_target_pairs={{0,3},{1,0},{2,1},{3,2},{4,7},{5,4},{6,5},{7,6},{8,11},{9,8},{10,9... | collective-permute-start | bytes 159752 | tf_op jit(solution)/shard_map/ppermute | solution.py:273
  16.4 1.1 %collective-permute-done.1.refs_2_ = bf16[208,128]{1,0:T(8,128)(2,1)S(1)} collective-permute-done((bf16[208,128]{1,0:T(8,128)(2,1)}, bf16[208,128]{1,0:T(8,128)(2,1)S(1)}, u32[]{:S(2)}, u32[]{:S(2)}) %collective-permute-start.1) | collective-permute-done | bytes 53280 | tf_op jit(solution)/shard_map/ppermute | solution.py:273
  17.4 1.5 %collective-permute-done.2.refs_3_ = bf16[208,128]{1,0:T(8,128)(2,1)S(1)} collective-permute-done((bf16[208,128]{1,0:T(8,128)(2,1)}, bf16[208,128]{1,0:T(8,128)(2,1)S(1)}, u32[]{:S(2)}, u32[]{:S(2)}) %collective-permute-start.2) | collective-permute-done | bytes 53280 | tf_op jit(solution)/shard_map/ppermute | solution.py:273
  18.9 0.6 %copy-done.10 = bf16[208,128]{1,0:T(8,128)(2,1)} copy-done((bf16[208,128]{1,0:T(8,128)(2,1)}, bf16[208,128]{1,0:T(8,128)(2,1)S(1)}, u32[]{:S(2)}) %copy-start.10) | copy-done | bytes 53272
  19.6 1.5 %join.1 = bf16[128,128]{1,0:T(8,128)(2,1)} custom-call(bf16[208,128]{1,0:T(8,128)(2,1)} %get-tuple-element.6.refs_0_, bf16[208,128]{1,0:T(8,128)(2,1)} %copy-done.8, bf16[208,128]{1,0:T(8,128)(2,1)} %copy-done.9, bf16[208,128]{1,0:T(8,128)(2,1)} %copy-done.10), custom_call_target="tpu_custom_call" | custom-call | tf_op jit(solution)/shard_map/join/pallas_call | solution.py:165
  21.1 1.6 %collective-permute-start.3 = (bf16[128,128]{1,0:T(8,128)(2,1)}, bf16[128,128]{1,0:T(8,128)(2,1)S(1)}, u32[]{:S(2)}, u32[]{:S(2)}) collective-permute-start(bf16[128,128]{1,0:T(8,128)(2,1)} %join.1), channel_id=1, source_target_pairs={{0,8},{4,12},{8,16},{12,20},{16,24},{20,28},{24,0},{28,4},{1,9},{5... | collective-permute-start | bytes 98312 | tf_op jit(solution)/shard_map/ppermute | solution.py:276
  22.7 2.6 %collective-permute-start.4 = (bf16[128,128]{1,0:T(8,128)(2,1)}, bf16[128,128]{1,0:T(8,128)(2,1)S(1)}, u32[]{:S(2)}, u32[]{:S(2)}) collective-permute-start(bf16[128,128]{1,0:T(8,128)(2,1)} %join.1), channel_id=1, source_target_pairs={{0,16},{4,20},{8,24},{12,28},{16,0},{20,4},{24,8},{28,12},{1,17},{... | collective-permute-start | bytes 98312 | tf_op jit(solution)/shard_map/ppermute | solution.py:276
  25.3 1.4 %collective-permute-start.5 = (bf16[128,128]{1,0:T(8,128)(2,1)}, bf16[128,128]{1,0:T(8,128)(2,1)S(1)}, u32[]{:S(2)}, u32[]{:S(2)}) collective-permute-start(bf16[128,128]{1,0:T(8,128)(2,1)} %join.1), channel_id=1, source_target_pairs={{0,24},{4,28},{8,0},{12,4},{16,8},{20,12},{24,16},{28,20},{1,25},{... | collective-permute-start | bytes 98312 | tf_op jit(solution)/shard_map/ppermute | solution.py:276
  27.0 0.7 %collective-permute-done.4 = bf16[128,128]{1,0:T(8,128)(2,1)S(1)} collective-permute-done((bf16[128,128]{1,0:T(8,128)(2,1)}, bf16[128,128]{1,0:T(8,128)(2,1)S(1)}, u32[]{:S(2)}, u32[]{:S(2)}) %collective-permute-start.4) | collective-permute-done | bytes 32800 | tf_op jit(solution)/shard_map/ppermute | solution.py:276
  27.7 1.7 %collective-permute-done.5 = bf16[128,128]{1,0:T(8,128)(2,1)S(1)} collective-permute-done((bf16[128,128]{1,0:T(8,128)(2,1)}, bf16[128,128]{1,0:T(8,128)(2,1)S(1)}, u32[]{:S(2)}, u32[]{:S(2)}) %collective-permute-start.5) | collective-permute-done | bytes 32800 | tf_op jit(solution)/shard_map/ppermute | solution.py:276
  29.4 0.8 %pad_maximum_fusion.refs_0_ = bf16[512,128]{1,0:T(8,128)(2,1)S(1)} fusion(bf16[128,128]{1,0:T(8,128)(2,1)S(1)} %collective-permute-done.5, bf16[128,128]{1,0:T(8,128)(2,1)S(1)} %collective-permute-done.4, bf16[128,128]{1,0:T(8,128)(2,1)S(1)} %collective-permute-done.3, bf16[128,128]{1,0:T(8,128)(2,1)} %join.1), kind=kLoop, calls=%fused_computation | loop fusion | flops 524288 | bytes 262144 | tf_op jit(solution)/shard_map/concatenate | solution.py:285
  30.2 1.4 %collective-permute-start.6 = (bf16[512,128]{1,0:T(8,128)(2,1)S(1)}, bf16[512,128]{1,0:T(8,128)(2,1)S(1)}, u32[]{:S(2)}, u32[]{:S(2)}) collective-permute-start(bf16[512,128]{1,0:T(8,128)(2,1)S(1)} %pad_maximum_fusion.refs_0_), channel_id=1, source_target_pairs={{0,1},{1,2},{2,3},{3,0},{4,5},{5,6},{6,7},{7,4},{8,9},{9,10},{10,1... | collective-permute-start | bytes 393224 | tf_op jit(solution)/shard_map/ppermute | solution.py:273
  31.6 1.5 %collective-permute-start.7 = (bf16[512,128]{1,0:T(8,128)(2,1)S(1)}, bf16[512,128]{1,0:T(8,128)(2,1)S(1)}, u32[]{:S(2)}, u32[]{:S(2)}) collective-permute-start(bf16[512,128]{1,0:T(8,128)(2,1)S(1)} %pad_maximum_fusion.refs_0_), channel_id=1, source_target_pairs={{0,2},{1,3},{2,0},{3,1},{4,6},{5,7},{6,4},{7,5},{8,10},{9,11},{10,... | collective-permute-start | bytes 393224 | tf_op jit(solution)/shard_map/ppermute | solution.py:273
  33.1 0.5 %collective-permute-start.8 = (bf16[512,128]{1,0:T(8,128)(2,1)S(1)}, bf16[512,128]{1,0:T(8,128)(2,1)S(1)}, u32[]{:S(2)}, u32[]{:S(2)}) collective-permute-start(bf16[512,128]{1,0:T(8,128)(2,1)S(1)} %pad_maximum_fusion.refs_0_), channel_id=1, source_target_pairs={{0,3},{1,0},{2,1},{3,2},{4,7},{5,4},{6,5},{7,6},{8,11},{9,8},{10,9... | collective-permute-start | bytes 393224 | tf_op jit(solution)/shard_map/ppermute | solution.py:273
  33.7 0.9 %copy.11 = bf16[128,128]{0,1:T(8,128)(2,1)S(1)} copy(bf16[128,128]{1,0:T(8,128)(2,1)} %join.1) | data formatting | bytes 65536 | tf_op jit(solution)/shard_map/join/pallas_call | solution.py:165
  34.6 1.6 %collective-permute-done.6.refs_1_ = bf16[512,128]{1,0:T(8,128)(2,1)S(1)} collective-permute-done((bf16[512,128]{1,0:T(8,128)(2,1)S(1)}, bf16[512,128]{1,0:T(8,128)(2,1)S(1)}, u32[]{:S(2)}, u32[]{:S(2)}) %collective-permute-start.6) | collective-permute-done | bytes 131104 | tf_op jit(solution)/shard_map/ppermute | solution.py:273
  36.4 1.1 %collective-permute-done.7.refs_2_ = bf16[512,128]{1,0:T(8,128)(2,1)S(1)} collective-permute-done((bf16[512,128]{1,0:T(8,128)(2,1)S(1)}, bf16[512,128]{1,0:T(8,128)(2,1)S(1)}, u32[]{:S(2)}, u32[]{:S(2)}) %collective-permute-start.7) | collective-permute-done | bytes 131104 | tf_op jit(solution)/shard_map/ppermute | solution.py:273
  39.3 0.9 %reshape.27 = f32[16,4096]{1,0:T(8,128)} reshape(f32[16,64,64]{2,1,0:T(8,128)S(1)} %fusion) | data formatting | bytes 524288 | tf_op jit(solution)/shard_map/reshape | solution.py:305
  40.3 0.6 %copy-done.4 = bf16[512,128]{1,0:T(8,128)(2,1)} copy-done((bf16[512,128]{1,0:T(8,128)(2,1)}, bf16[512,128]{1,0:T(8,128)(2,1)S(1)}, u32[]{:S(2)}) %copy-start.4) | copy-done | bytes 131096
  40.9 0.7 %copy-done.7 = bf16[512,128]{1,0:T(8,128)(2,1)} copy-done((bf16[512,128]{1,0:T(8,128)(2,1)}, bf16[512,128]{1,0:T(8,128)(2,1)S(1)}, u32[]{:S(2)}) %copy-start.7) | copy-done | bytes 131096
  41.6 5.5 %gram.1 = f32[1024,512]{1,0:T(8,128)} custom-call(bf16[512,128]{1,0:T(8,128)(2,1)} %copy-done, bf16[512,128]{1,0:T(8,128)(2,1)} %copy-done.1, bf16[512,128]{1,0:T(8,128)(2,1)} %copy-done.2, bf16[512,128]{1,0:T(8,128)(2,1)} %copy-done.3, bf16[512,128]{1,0:T(8,128)(2,1)} %copy-done.4, bf16[512,128]{1,0:T(8,128)(2,1)} %copy-done.5, bf16[512,128]{1,0:T(8,128)(2,1)} %copy-done.6, ...), custom_call_target="tpu_custom_call" | custom-call | tf_op jit(solution)/shard_map/gram/pallas_call | solution.py:238
  (44 shorter events, 2.8 us)
Async XLA Ops:
  10.1 6.3 %collective-permute-start = (bf16[208,128]{1,0:T(8,128)(2,1)}, bf16[208,128]{1,0:T(8,128)(2,1)S(1)}, u32[]{:S(2)}, u32[]{:S(2)}) collective-permute-start(bf16[208,128]{1,0:T(8,128)(2,1)} %get-tuple-element.7), channel_id=1, source_target_pairs={{0,1},{1,2},{2,3},{3,0},{4,5},{5,6},{6,7},{7,4},{8,9},{9,10},{10,1... | collective-permute-start | bytes 159752 | tf_op jit(solution)/shard_map/ppermute | solution.py:273
  13.1 4.3 %collective-permute-start.1 = (bf16[208,128]{1,0:T(8,128)(2,1)}, bf16[208,128]{1,0:T(8,128)(2,1)S(1)}, u32[]{:S(2)}, u32[]{:S(2)}) collective-permute-start(bf16[208,128]{1,0:T(8,128)(2,1)} %get-tuple-element.8), channel_id=1, source_target_pairs={{0,2},{1,3},{2,0},{3,1},{4,6},{5,7},{6,4},{7,5},{8,10},{9,11},{10,... | collective-permute-start | bytes 159752 | tf_op jit(solution)/shard_map/ppermute | solution.py:273
  14.6 4.3 %collective-permute-start.2 = (bf16[208,128]{1,0:T(8,128)(2,1)}, bf16[208,128]{1,0:T(8,128)(2,1)S(1)}, u32[]{:S(2)}, u32[]{:S(2)}) collective-permute-start(bf16[208,128]{1,0:T(8,128)(2,1)} %get-tuple-element.9), channel_id=1, source_target_pairs={{0,3},{1,0},{2,1},{3,2},{4,7},{5,4},{6,5},{7,6},{8,11},{9,8},{10,9... | collective-permute-start | bytes 159752 | tf_op jit(solution)/shard_map/ppermute | solution.py:273
  16.4 2.6 %copy-start.8 = (bf16[208,128]{1,0:T(8,128)(2,1)}, bf16[208,128]{1,0:T(8,128)(2,1)S(1)}, u32[]{:S(2)}) copy-start(bf16[208,128]{1,0:T(8,128)(2,1)S(1)} %collective-permute-done.refs_1_) | copy-start | bytes 159748
  17.4 1.5 %copy-start.9 = (bf16[208,128]{1,0:T(8,128)(2,1)}, bf16[208,128]{1,0:T(8,128)(2,1)S(1)}, u32[]{:S(2)}) copy-start(bf16[208,128]{1,0:T(8,128)(2,1)S(1)} %collective-permute-done.1.refs_2_) | copy-start | bytes 159748
  18.9 0.6 %copy-start.10 = (bf16[208,128]{1,0:T(8,128)(2,1)}, bf16[208,128]{1,0:T(8,128)(2,1)S(1)}, u32[]{:S(2)}) copy-start(bf16[208,128]{1,0:T(8,128)(2,1)S(1)} %collective-permute-done.2.refs_3_) | copy-start | bytes 159748
  21.1 5.9 %collective-permute-start.3 = (bf16[128,128]{1,0:T(8,128)(2,1)}, bf16[128,128]{1,0:T(8,128)(2,1)S(1)}, u32[]{:S(2)}, u32[]{:S(2)}) collective-permute-start(bf16[128,128]{1,0:T(8,128)(2,1)} %join.1), channel_id=1, source_target_pairs={{0,8},{4,12},{8,16},{12,20},{16,24},{20,28},{24,0},{28,4},{1,9},{5... | collective-permute-start | bytes 98312 | tf_op jit(solution)/shard_map/ppermute | solution.py:276
  22.7 5.0 %collective-permute-start.4 = (bf16[128,128]{1,0:T(8,128)(2,1)}, bf16[128,128]{1,0:T(8,128)(2,1)S(1)}, u32[]{:S(2)}, u32[]{:S(2)}) collective-permute-start(bf16[128,128]{1,0:T(8,128)(2,1)} %join.1), channel_id=1, source_target_pairs={{0,16},{4,20},{8,24},{12,28},{16,0},{20,4},{24,8},{28,12},{1,17},{... | collective-permute-start | bytes 98312 | tf_op jit(solution)/shard_map/ppermute | solution.py:276
  25.3 4.1 %collective-permute-start.5 = (bf16[128,128]{1,0:T(8,128)(2,1)}, bf16[128,128]{1,0:T(8,128)(2,1)S(1)}, u32[]{:S(2)}, u32[]{:S(2)}) collective-permute-start(bf16[128,128]{1,0:T(8,128)(2,1)} %join.1), channel_id=1, source_target_pairs={{0,24},{4,28},{8,0},{12,4},{16,8},{20,12},{24,16},{28,20},{1,25},{... | collective-permute-start | bytes 98312 | tf_op jit(solution)/shard_map/ppermute | solution.py:276
  30.2 10.1 %copy-start = (bf16[512,128]{1,0:T(8,128)(2,1)}, bf16[512,128]{1,0:T(8,128)(2,1)S(1)}, u32[]{:S(2)}) copy-start(bf16[512,128]{1,0:T(8,128)(2,1)S(1)} %pad_maximum_fusion.refs_0_) | copy-start | bytes 393220
  30.2 6.0 %collective-permute-start.6 = (bf16[512,128]{1,0:T(8,128)(2,1)S(1)}, bf16[512,128]{1,0:T(8,128)(2,1)S(1)}, u32[]{:S(2)}, u32[]{:S(2)}) collective-permute-start(bf16[512,128]{1,0:T(8,128)(2,1)S(1)} %pad_maximum_fusion.refs_0_), channel_id=1, source_target_pairs={{0,1},{1,2},{2,3},{3,0},{4,5},{5,6},{6,7},{7,4},{8,9},{9,10},{10,1... | collective-permute-start | bytes 393224 | tf_op jit(solution)/shard_map/ppermute | solution.py:273
  31.6 5.9 %collective-permute-start.7 = (bf16[512,128]{1,0:T(8,128)(2,1)S(1)}, bf16[512,128]{1,0:T(8,128)(2,1)S(1)}, u32[]{:S(2)}, u32[]{:S(2)}) collective-permute-start(bf16[512,128]{1,0:T(8,128)(2,1)S(1)} %pad_maximum_fusion.refs_0_), channel_id=1, source_target_pairs={{0,2},{1,3},{2,0},{3,1},{4,6},{5,7},{6,4},{7,5},{8,10},{9,11},{10,... | collective-permute-start | bytes 393224 | tf_op jit(solution)/shard_map/ppermute | solution.py:273
  33.1 5.0 %collective-permute-start.8 = (bf16[512,128]{1,0:T(8,128)(2,1)S(1)}, bf16[512,128]{1,0:T(8,128)(2,1)S(1)}, u32[]{:S(2)}, u32[]{:S(2)}) collective-permute-start(bf16[512,128]{1,0:T(8,128)(2,1)S(1)} %pad_maximum_fusion.refs_0_), channel_id=1, source_target_pairs={{0,3},{1,0},{2,1},{3,2},{4,7},{5,4},{6,5},{7,6},{8,11},{9,8},{10,9... | collective-permute-start | bytes 393224 | tf_op jit(solution)/shard_map/ppermute | solution.py:273
  34.5 5.6 %collective-permute-start.9 = (bf16[512,128]{1,0:T(8,128)(2,1)S(1)}, bf16[512,128]{1,0:T(8,128)(2,1)S(1)}, u32[]{:S(2)}, u32[]{:S(2)}) collective-permute-start(bf16[512,128]{1,0:T(8,128)(2,1)S(1)} %pad_maximum_fusion.refs_0_), channel_id=1, source_target_pairs={{0,4},{4,0},{8,12},{12,8},{16,20},{20,16},{24,28},{28,24},{1,5},{5... | collective-permute-start | bytes 393224 | tf_op jit(solution)/shard_map/ppermute | solution.py:279
  36.2 4.1 %copy-start.1 = (bf16[512,128]{1,0:T(8,128)(2,1)}, bf16[512,128]{1,0:T(8,128)(2,1)S(1)}, u32[]{:S(2)}) copy-start(bf16[512,128]{1,0:T(8,128)(2,1)S(1)} %collective-permute-done.6.refs_1_) | copy-start | bytes 393220
  37.5 2.8 %copy-start.2 = (bf16[512,128]{1,0:T(8,128)(2,1)}, bf16[512,128]{1,0:T(8,128)(2,1)S(1)}, u32[]{:S(2)}) copy-start(bf16[512,128]{1,0:T(8,128)(2,1)S(1)} %collective-permute-done.7.refs_2_) | copy-start | bytes 393220
  38.1 2.2 %copy-start.3 = (bf16[512,128]{1,0:T(8,128)(2,1)}, bf16[512,128]{1,0:T(8,128)(2,1)S(1)}, u32[]{:S(2)}) copy-start(bf16[512,128]{1,0:T(8,128)(2,1)S(1)} %collective-permute-done.8.refs_3_) | copy-start | bytes 393220
  38.3 1.9 %collective-permute-start.10 = (bf16[512,128]{1,0:T(8,128)(2,1)S(1)}, bf16[512,128]{1,0:T(8,128)(2,1)S(1)}, u32[]{:S(2)}, u32[]{:S(2)}) collective-permute-start(bf16[512,128]{1,0:T(8,128)(2,1)S(1)} %collective-permute-done.6.refs_1_), channel_id=1, source_target_pairs={{0,4},{4,0},{8,12},{12,8},{16,20},{20,16},{24,28},{28,24},{1,5},{5... | collective-permute-start | bytes 393224 | tf_op jit(solution)/shard_map/ppermute | solution.py:279
  38.4 1.8 %collective-permute-start.11 = (bf16[512,128]{1,0:T(8,128)(2,1)S(1)}, bf16[512,128]{1,0:T(8,128)(2,1)S(1)}, u32[]{:S(2)}, u32[]{:S(2)}) collective-permute-start(bf16[512,128]{1,0:T(8,128)(2,1)S(1)} %collective-permute-done.7.refs_2_), channel_id=1, source_target_pairs={{0,4},{4,0},{8,12},{12,8},{16,20},{20,16},{24,28},{28,24},{1,5},{5... | collective-permute-start | bytes 393224 | tf_op jit(solution)/shard_map/ppermute | solution.py:279
  38.9 1.3 %collective-permute-start.12 = (bf16[512,128]{1,0:T(8,128)(2,1)S(1)}, bf16[512,128]{1,0:T(8,128)(2,1)S(1)}, u32[]{:S(2)}, u32[]{:S(2)}) collective-permute-start(bf16[512,128]{1,0:T(8,128)(2,1)S(1)} %collective-permute-done.8.refs_3_), channel_id=1, source_target_pairs={{0,4},{4,0},{8,12},{12,8},{16,20},{20,16},{24,28},{28,24},{1,5},{5... | collective-permute-start | bytes 393224 | tf_op jit(solution)/shard_map/ppermute | solution.py:279
  40.2 0.7 %copy-start.4 = (bf16[512,128]{1,0:T(8,128)(2,1)}, bf16[512,128]{1,0:T(8,128)(2,1)S(1)}, u32[]{:S(2)}) copy-start(bf16[512,128]{1,0:T(8,128)(2,1)S(1)} %collective-permute-done.9.refs_4_) | copy-start | bytes 393220
  40.2 0.7 %copy-start.5 = (bf16[512,128]{1,0:T(8,128)(2,1)}, bf16[512,128]{1,0:T(8,128)(2,1)S(1)}, u32[]{:S(2)}) copy-start(bf16[512,128]{1,0:T(8,128)(2,1)S(1)} %collective-permute-done.10.refs_5_) | copy-start | bytes 393220
  40.2 0.7 %copy-start.6 = (bf16[512,128]{1,0:T(8,128)(2,1)}, bf16[512,128]{1,0:T(8,128)(2,1)S(1)}, u32[]{:S(2)}) copy-start(bf16[512,128]{1,0:T(8,128)(2,1)S(1)} %collective-permute-done.11.refs_6_) | copy-start | bytes 393220
  40.9 0.7 %copy-start.7 = (bf16[512,128]{1,0:T(8,128)(2,1)}, bf16[512,128]{1,0:T(8,128)(2,1)S(1)}, u32[]{:S(2)}) copy-start(bf16[512,128]{1,0:T(8,128)(2,1)S(1)} %collective-permute-done.12.refs_7_) | copy-start | bytes 393220

commit v2 on v1

--- a/solution.py
+++ b/solution.py
@@ -10,9 +10,11 @@
 SEQ = 8
 LOG2E = 1.4426950408889634
 LANES = 128
-CHUNK = 1024
+CHUNK = 3456
 SUB = 256
 STAT = 16
+AHEAD = 20
+FIRST = 1152
 F32 = jnp.float32
 BF16 = jnp.bfloat16
 
@@ -21,41 +23,53 @@
     return (a + b - 1) // b
 
 
-def _sizes(total, step):
+def _sizes(total, step, first=None):
     out = []
     start = 0
     while start < total:
-        out.append((start, min(step, total - start)))
-        start += step
+        size = min(first if first and not start else step, total - start)
+        out.append((start, size))
+        start += size
     return out
+
+
+def _partner(i, k, n):
+    return i ^ k if n & (n - 1) == 0 else (i + k) % n
+
+
+def _on_chip(arrays):
+    return [pltpu.with_memory_space_constraint(a, pltpu.VMEM) for a in arrays]
 
 
 def _local_kernel(
     logits_hbm, labels_hbm, act_hbm, pin_hbm, pout_hbm, *rest, groups, vocab, tokens, width, k_in, k_out
 ):
     outs = rest[:groups]
-    buf, lab, act, pin, pext, acc, plab, top, msg, sem, lsem = rest[groups:]
-    copies = [
-        pltpu.make_async_copy(pin_hbm, pin, sem.at[0]),
-        pltpu.make_async_copy(act_hbm, act, sem.at[1]),
-        pltpu.make_async_copy(pout_hbm, pext.at[0:k_out, :], sem.at[2]),
-        pltpu.make_async_copy(labels_hbm, lab, sem.at[3]),
-    ]
-    for c in copies:
-        c.start()
-    chunks = _sizes(vocab, CHUNK)
-    loads = []
+    buf, lab, act, pin, pext, wide, acc, plab, top, msg, sem, lsem, psem = rest[groups:]
+    chunks = _sizes(vocab, CHUNK, FIRST)
+    queue, loads, pout_loads = [], [], []
+    label_load = pltpu.make_async_copy(labels_hbm, lab, sem.at[0])
+    act_load = pltpu.make_async_copy(act_hbm, act, sem.at[1])
+    pin_load = pltpu.make_async_copy(pin_hbm, pin, sem.at[2])
     for n, (start, size) in enumerate(chunks):
-        c = pltpu.make_async_copy(logits_hbm.at[start : start + size, :], buf.at[start : start + size, :], lsem.at[n])
-        c.start()
-        loads.append(c)
+        cols = slice(start, start + size)
+        loads.append(pltpu.make_async_copy(logits_hbm.at[cols, :], buf.at[cols, :], lsem.at[n]))
+        pout_loads.append(pltpu.make_async_copy(pout_hbm.at[:, cols], pext.at[0:k_out, cols], psem.at[n]))
+        queue.append((loads[n], pout_loads[n], label_load) if n == 0 else (loads[n], pout_loads[n]))
+        if n == min(3, len(chunks) - 1):
+            queue.append((act_load, pin_load))
+    started = 0
+
+    def start_next(count):
+        nonlocal started
+        for group in queue[started : started + count]:
+            for c in group:
+                c.start()
+        started += count
+
+    start_next(AHEAD)
     mine = lax.axis_index("fsdp")
-    copies[0].wait()
-    copies[1].wait()
-    left = lax.dot_general(pin[...], act[...], (((1,), (1,)), ((), ())), preferred_element_type=F32)
-    msg[0:k_in, :] = left.astype(BF16)
-    copies[2].wait()
-    copies[3].wait()
+    label_load.wait()
     pext[k_out : k_out + STAT, :] = jnp.ones((STAT, vocab), BF16)
     acc[...] = jnp.zeros_like(acc)
     plab[...] = jnp.zeros_like(plab)
@@ -68,6 +82,14 @@
 
     for n, (start, size) in enumerate(chunks):
         loads[n].wait()
+        pout_loads[n].wait()
+        start_next(1)
+        if n == min(2, len(chunks) - 1):
+            start_next(len(queue))
+            act_load.wait()
+            pin_load.wait()
+            left = lax.dot_general(pin[...], act[...], (((1,), (1,)), ((), ())), preferred_element_type=F32)
+            msg[0:k_in, :] = left.astype(BF16)
         peak = None
         for r, h in _sizes(size, 16):
             part = buf[start + r : start + r + h, :]
@@ -83,16 +105,16 @@
             expo = jnp.exp2((part - new) * LOG2E).astype(BF16)
             total = total + jnp.dot(pext[:, start + r : start + r + h], expo, preferred_element_type=F32)
         acc[...] = total
+        blocks = _sizes(size, LANES)
+        for r, h in blocks:
+            wide[:, r : r + h] = pext[0:k_out, start + r : start + r + h].astype(F32)
         for t in range(_cdiv(tokens, LANES)):
             cols = slice(t * LANES, (t + 1) * LANES)
             which = jnp.broadcast_to(block[:, cols], (k_out, LANES))
             index = jnp.broadcast_to(lane[:, cols], (k_out, LANES))
             found = plab[:, cols]
-            for r, h in _sizes(size, LANES):
-                tile = pext[0:k_out, start + r : start + r + h].astype(F32)
-                if h < LANES:
-                    tile = jnp.concatenate([tile, jnp.zeros((k_out, LANES - h), F32)], axis=1)
-                got = jnp.take_along_axis(tile, index, axis=1)
+            for r, h in blocks:
+                got = jnp.take_along_axis(wide[:, r : r + LANES], index, axis=1)
                 found = jnp.where(which == (start + r) // LANES, got, found)
             plab[:, cols] = found
 
@@ -105,13 +127,13 @@
     msg[k_in + 2 * k_out :, :] = stat.astype(BF16)
     share = tokens // groups
     examples = tokens // SEQ
-    src = lax.broadcasted_iota(jnp.int32, (tokens, tokens), 0)
-    dst = lax.broadcasted_iota(jnp.int32, (tokens, tokens), 1) + mine * share
-    dst = jnp.where(dst >= tokens, dst - tokens, dst)
-    want = jnp.bitwise_and(dst, examples - 1) * SEQ + lax.shift_right_arithmetic(dst, examples.bit_length() - 1)
-    moved = jnp.dot(msg[...], jnp.where(src == want, 1.0, 0.0).astype(BF16), preferred_element_type=F32).astype(BF16)
+    src = lax.broadcasted_iota(jnp.int32, (tokens, share), 0)
+    place = lax.broadcasted_iota(jnp.int32, (tokens, share), 1)
     for k in range(groups):
-        outs[k][...] = moved[:, k * share : (k + 1) * share]
+        dst = place + _partner(mine, k, groups) * share
+        want = jnp.bitwise_and(dst, examples - 1) * SEQ + lax.shift_right_arithmetic(dst, examples.bit_length() - 1)
+        pick = jnp.where(src == want, 1.0, 0.0).astype(BF16)
+        outs[k][...] = jnp.dot(msg[...], pick, preferred_element_type=F32).astype(BF16)
 
 
 def _local(logits, labels, act, pin, pout, groups):
@@ -120,13 +142,13 @@
     k_out = pout.shape[0]
     rows = k_in + 2 * k_out + STAT
     share = tokens // groups
-    n_chunks = _cdiv(vocab, CHUNK)
+    n_chunks = len(_sizes(vocab, CHUNK, FIRST))
     any_spec = pl.BlockSpec(memory_space=pl.ANY)
     return pl.pallas_call(
         functools.partial(
             _local_kernel, groups=groups, vocab=vocab, tokens=tokens, width=width, k_in=k_in, k_out=k_out
         ),
-        out_shape=[jax.ShapeDtypeStruct((rows, share), BF16)] * groups,
+        out_shape=[pltpu.VMEM((rows, share), BF16)] * groups,
         in_specs=[any_spec] * 5,
         out_specs=[pl.BlockSpec(memory_space=pltpu.VMEM)] * groups,
         scratch_shapes=[
@@ -135,11 +157,13 @@
             pltpu.VMEM((tokens, width), BF16),
             pltpu.VMEM((k_in, width), BF16),
             pltpu.VMEM((k_out + STAT, vocab), BF16),
+            pltpu.VMEM((k_out, CHUNK), F32),
             pltpu.VMEM((k_out + STAT, tokens), F32),
             pltpu.VMEM((k_out, tokens), F32),
             pltpu.VMEM((1, tokens), F32),
             pltpu.VMEM((rows, tokens), BF16),
-            pltpu.SemaphoreType.DMA((4,)),
+            pltpu.SemaphoreType.DMA((3,)),
+            pltpu.SemaphoreType.DMA((n_chunks,)),
             pltpu.SemaphoreType.DMA((n_chunks,)),
         ],
         name="local_pass",
@@ -164,11 +188,11 @@
 def _join(parts, k_in, k_out):
     return pl.pallas_call(
         functools.partial(_join_kernel, k_in=k_in, k_out=k_out),
-        out_shape=jax.ShapeDtypeStruct((k_in + k_out, parts[0].shape[1]), BF16),
+        out_shape=pltpu.VMEM((k_in + k_out, parts[0].shape[1]), BF16),
         in_specs=[pl.BlockSpec(memory_space=pltpu.VMEM)] * len(parts),
         out_specs=pl.BlockSpec(memory_space=pltpu.VMEM),
         name="join",
-    )(*parts)
+    )(*_on_chip(parts))
 
 
 def _gram_body(x, out_hbm, frow, fcol, res, sem, n_row, n_col, k_out):
@@ -257,7 +281,7 @@
             pltpu.SemaphoreType.DMA((8,)),
         ],
         name="gram",
-    )(*ins)
+    )(*_on_chip(ins))
 
 
 def body(logits, labels, activations, proj_in, proj_out):
@@ -270,20 +294,23 @@
     share = tokens // n_f
 
     def along_f(a, k):
-        return lax.ppermute(a, "fsdp", [(i, (i + k) % n_f) for i in range(n_f)])
+        return lax.ppermute(a, "fsdp", [(i, _partner(i, k, n_f)) for i in range(n_f)])
 
     def along_z(a, k):
-        return lax.ppermute(a, "dp", [(i, (i + 2 * k) % n_d) for i in range(n_d)])
+        return lax.ppermute(a, "dp", [(i, 2 * _partner(i // 2, k, n_d // 2) + i % 2) for i in range(n_d)])
+
+    def far_first(n):
+        return range(n - 1, 0, -1)
 
     def other_core(a):
         return lax.ppermute(a, "dp", [(i, i ^ 1) for i in range(n_d)])
 
     parts = _local(logits.T, labels.reshape(1, tokens), activations, proj_in.T, proj_out.T, n_f)
-    parts = [parts[0]] + [along_f(parts[k], k) for k in range(1, n_f)]
+    parts = [parts[0]] + [along_f(parts[k], k) for k in far_first(n_f)]
     joined = _join(parts, k_in, k_out)
     n_z = n_d // 2
-    column = jnp.concatenate([joined] + [along_z(joined, k) for k in range(1, n_z)], axis=0)
-    own = [column] + [along_f(column, k) for k in range(1, n_f)]
+    column = jnp.concatenate([joined] + [along_z(joined, k) for k in far_first(n_z)], axis=0)
+    own = [column] + [along_f(column, k) for k in far_first(n_f)]
     other = [other_core(a) for a in own]
 
     mine = lax.axis_index("fsdp")
@@ -295,7 +322,7 @@
             pieces.append(lax.dynamic_slice_in_dim(part, mine * own_examples, own_examples, 2))
         group = jnp.concatenate(pieces, axis=1)
     else:
-        order = [(mine - k) % n_f for k in range(n_f)]
+        order = [mine] + [_partner(mine, k, n_f) if n_f & (n_f - 1) == 0 else (mine - k) % n_f for k in far_first(n_f)]
         whole = jnp.zeros((n_f, rows, share), BF16)
         for k, a in enumerate(own):
             whole = lax.dynamic_update_slice(whole, a[:rows][None], (order[k], 0, 0))
@@ -309,7 +336,7 @@
     if share == LANES and 2 * examples == LANES and n_row % 8 == 0 and n_col % 8 == 0:
         gram = _gram(own + other, n_z, examples, lanes, n_row, n_col, k_in, k_out)
     else:
-        order = [(mine - k) % n_f for k in range(n_f)]
+        order = [mine] + [_partner(mine, k, n_f) if n_f & (n_f - 1) == 0 else (mine - k) % n_f for k in far_first(n_f)]
         whole = jnp.zeros((n_f, 2, n_z, rows, share), BF16)
         for c, arrays in enumerate((own, other)):
             for k, a in enumerate(arrays):

time: 47.4 us -> 38.1 us (0.80)
  Pallas kernels: 16.4 us -> 10.6 us
  local copies, waits for them, and re-layouts: 4.12 us -> 1.4 us
  waiting for transfers between devices: 8.9 us -> 11.5 us
  starting transfers between devices: 15.7 us -> 13.4 us
  other arithmetic: 0.81 us -> 0.06 us
    pallas_call x1, Pallas kernels: 9.41 us -> 6.56 us  [_local(): pl.pallas_call(functools.partial(_local_kernel, groups=groups, vocab=voca...]
    ppermute x9, waiting for transfers between devices: 8.86 us -> 11.4 us  [the longest x6 7.42 us: along_f(): lax.ppermute(a, 'fsdp', [(i, _partner(i, k, n_f)) for i in range(n_f)])]
    ppermute x9, starting transfers between devices: 15 us -> 12.6 us  [the longest x6 8.19 us: along_f(): lax.ppermute(a, 'fsdp', [(i, _partner(i, k, n_f)) for i in range(n_f)])]
    unnamed x26 -> x4, local copies, waits for them, and re-layouts: 2 us -> 0.03 us
    pallas_call x1, Pallas kernels: 1.54 us -> 0.04 us  [_join(): pl.pallas_call(functools.partial(_join_kernel, k_in=k_in, k_out=k_out), o...]
    pallas_call x1, Pallas kernels: 5.45 us -> 4.01 us  [_gram(): pl.pallas_call(functools.partial(_gram_kernel, n_in=len(ins), blocks=bloc...]
    concatenate x1, other arithmetic: 0.77 us -> 0.01 us  [body(): jnp.concatenate([joined] + [along_z(joined, k) for k in far_first(n_z)],...]
    pallas_call x1, local copies, waits for them, and re-layouts: 0.86 us -> 0.11 us  [_join(): pl.pallas_call(functools.partial(_join_kernel, k_in=k_in, k_out=k_out), o...]
  transfers between devices with their start and end apart: 13 -> 13, of which waited for: 9 -> 8; matrix products, arithmetic and copies ran while one was open for 5% -> 5% of each run, Pallas kernels for 0% -> 0%
where the time goes in v2:
time: 38.1 us; the launch traced here: 38 us
  starting transfers between devices  13.4 us (35%)
  waiting for transfers between devices  11.5 us (30%)
  Pallas kernels  10.6 us (28%)
  local copies, waits for them, and re-layouts  1.4 us (4%)
  between operations  0.78 us (2%)
    ppermute x6, starting transfers between devices, along_f(): lax.ppermute(a, 'fsdp', [(i, _partner(i, k, n_f)) for i in range(n_f)])  8.19 us
    ppermute x6, waiting for transfers between devices, along_f(): lax.ppermute(a, 'fsdp', [(i, _partner(i, k, n_f)) for i in range(n_f)])  7.42 us
    pallas_call x1, Pallas kernels, _local(): pl.pallas_call(functools.partial(_local_kernel, groups=groups, vocab=voca...  6.56 us
    ppermute x3, starting transfers between devices, along_z(): lax.ppermute(a, 'dp', [(i, 2 * _partner(i // 2, k, n_d // 2) + i % 2) for...  4.45 us
    ppermute x3, waiting for transfers between devices, along_z(): lax.ppermute(a, 'dp', [(i, 2 * _partner(i // 2, k, n_d // 2) + i % 2) for...  4.02 us
    pallas_call x1, Pallas kernels, _gram(): pl.pallas_call(functools.partial(_gram_kernel, n_in=len(ins), blocks=bloc...  4.01 us
    reshape x1, local copies, waits for them, and re-layouts, body(): features = features.reshape(own_examples, k_in * k_out)  0.89 us
  transfers between devices with their start and end apart: 13, of which 8 were waited for; matrix products, arithmetic and copies ran while one was open for 5% of the time, Pallas kernels for 0%

profile of v2, /device:TPU:0, one launch (start us, length us, event | category | flops | bytes accessed | tf_op | source)
XLA Modules:
  0.0 38.0 jit_solution(4142154561455556090)
XLA Ops:
  0.6 6.6 %local_pass.1 = (bf16[208,128]{1,0:T(8,128)(2,1)S(1)}, bf16[208,128]{1,0:T(8,128)(2,1)S(1)}, bf16[208,128]{1,0:T(8,128)(2,1)S(1)}, bf16[208,128]{1,0:T(8,128)(2,1)S(1)}) custom-call(bf16[8000,512]{1,0:T(8,128)(2,1)} %bitcast.8, s32[1,512]{1,0:T(1,128)} %bitcast.15, bf16[512,1280]{1,0:T(8,128)(2,1)} %act_hbm.1, bf16[64,1280]{1,0:T(8,128)(2,1)} %bitcast.10, ...), custom_call_target="tpu_custom_call" | custom-call | tf_op jit(solution)/shard_map/local_pass/pallas_call | solution.py:147
  7.2 4.0 %collective-permute-start = (bf16[208,128]{1,0:T(8,128)(2,1)S(1)}, bf16[208,128]{1,0:T(8,128)(2,1)S(1)}, u32[]{:S(2)}, u32[]{:S(2)}) collective-permute-start(bf16[208,128]{1,0:T(8,128)(2,1)S(1)} %get-tuple-element.7), channel_id=1, source_target_pairs={{0,3},{1,2},{2,1},{3,0},{4,7},{5,6},{6,5},{7,4},{8,11},{9,10},{10,... | collective-permute-start | bytes 159752 | tf_op jit(solution)/shard_map/ppermute | solution.py:297
  11.2 0.5 %collective-permute-start.1 = (bf16[208,128]{1,0:T(8,128)(2,1)S(1)}, bf16[208,128]{1,0:T(8,128)(2,1)S(1)}, u32[]{:S(2)}, u32[]{:S(2)}) collective-permute-start(bf16[208,128]{1,0:T(8,128)(2,1)S(1)} %get-tuple-element.8), channel_id=1, source_target_pairs={{0,2},{1,3},{2,0},{3,1},{4,6},{5,7},{6,4},{7,5},{8,10},{9,11},{10,... | collective-permute-start | bytes 159752 | tf_op jit(solution)/shard_map/ppermute | solution.py:297
  11.7 0.1 collective-permute-start.2
  11.8 1.5 %collective-permute-done.refs_1_ = bf16[208,128]{1,0:T(8,128)(2,1)S(1)} collective-permute-done((bf16[208,128]{1,0:T(8,128)(2,1)S(1)}, bf16[208,128]{1,0:T(8,128)(2,1)S(1)}, u32[]{:S(2)}, u32[]{:S(2)}) %collective-permute-start) | collective-permute-done | bytes 53280 | tf_op jit(solution)/shard_map/ppermute | solution.py:297
  13.3 2.0 %collective-permute-done.1.refs_2_ = bf16[208,128]{1,0:T(8,128)(2,1)S(1)} collective-permute-done((bf16[208,128]{1,0:T(8,128)(2,1)S(1)}, bf16[208,128]{1,0:T(8,128)(2,1)S(1)}, u32[]{:S(2)}, u32[]{:S(2)}) %collective-permute-start.1) | collective-permute-done | bytes 53280 | tf_op jit(solution)/shard_map/ppermute | solution.py:297
  15.3 0.5 %collective-permute-done.2.refs_3_ = bf16[208,128]{1,0:T(8,128)(2,1)S(1)} collective-permute-done((bf16[208,128]{1,0:T(8,128)(2,1)S(1)}, bf16[208,128]{1,0:T(8,128)(2,1)S(1)}, u32[]{:S(2)}, u32[]{:S(2)}) %collective-permute-start.2) | collective-permute-done | bytes 53280 | tf_op jit(solution)/shard_map/ppermute | solution.py:297
  15.9 3.7 %collective-permute-start.3 = (bf16[128,128]{1,0:T(8,128)(2,1)S(1)}, bf16[128,128]{1,0:T(8,128)(2,1)S(1)}, u32[]{:S(2)}, u32[]{:S(2)}) collective-permute-start(bf16[128,128]{1,0:T(8,128)(2,1)S(1)} %join.1), channel_id=1, source_target_pairs={{0,24},{4,28},{8,16},{12,20},{16,8},{20,12},{24,0},{28,4},{1,25},{... | collective-permute-start | bytes 98312 | tf_op jit(solution)/shard_map/ppermute | solution.py:300
  19.5 0.8 %collective-permute-start.5 = (bf16[128,128]{1,0:T(8,128)(2,1)S(1)}, bf16[128,128]{1,0:T(8,128)(2,1)S(1)}, u32[]{:S(2)}, u32[]{:S(2)}) collective-permute-start(bf16[128,128]{1,0:T(8,128)(2,1)S(1)} %join.1), channel_id=1, source_target_pairs={{0,8},{4,12},{8,0},{12,4},{16,24},{20,28},{24,16},{28,20},{1,9},{5... | collective-permute-start | bytes 98312 | tf_op jit(solution)/shard_map/ppermute | solution.py:300
  20.3 1.4 %collective-permute-done.3 = bf16[128,128]{1,0:T(8,128)(2,1)S(1)} collective-permute-done((bf16[128,128]{1,0:T(8,128)(2,1)S(1)}, bf16[128,128]{1,0:T(8,128)(2,1)S(1)}, u32[]{:S(2)}, u32[]{:S(2)}) %collective-permute-start.3) | collective-permute-done | bytes 32800 | tf_op jit(solution)/shard_map/ppermute | solution.py:300
  21.8 2.6 %collective-permute-done.4 = bf16[128,128]{1,0:T(8,128)(2,1)S(1)} collective-permute-done((bf16[128,128]{1,0:T(8,128)(2,1)S(1)}, bf16[128,128]{1,0:T(8,128)(2,1)S(1)}, u32[]{:S(2)}, u32[]{:S(2)}) %collective-permute-start.4) | collective-permute-done | bytes 32800 | tf_op jit(solution)/shard_map/ppermute | solution.py:300
  24.4 1.6 %collective-permute-start.6 = (bf16[512,128]{1,0:T(8,128)(2,1)S(1)}, bf16[512,128]{1,0:T(8,128)(2,1)S(1)}, u32[]{:S(2)}, u32[]{:S(2)}) collective-permute-start(bf16[512,128]{1,0:T(8,128)(2,1)S(1)} %pad_maximum_fusion.refs_0_), channel_id=1, source_target_pairs={{0,3},{1,2},{2,1},{3,0},{4,7},{5,6},{6,5},{7,4},{8,11},{9,10},{10,... | collective-permute-start | bytes 393224 | tf_op jit(solution)/shard_map/ppermute | solution.py:297
  25.9 0.5 %collective-permute-start.7 = (bf16[512,128]{1,0:T(8,128)(2,1)S(1)}, bf16[512,128]{1,0:T(8,128)(2,1)S(1)}, u32[]{:S(2)}, u32[]{:S(2)}) collective-permute-start(bf16[512,128]{1,0:T(8,128)(2,1)S(1)} %pad_maximum_fusion.refs_0_), channel_id=1, source_target_pairs={{0,2},{1,3},{2,0},{3,1},{4,6},{5,7},{6,4},{7,5},{8,10},{9,11},{10,... | collective-permute-start | bytes 393224 | tf_op jit(solution)/shard_map/ppermute | solution.py:297
  26.4 1.5 %collective-permute-start.8 = (bf16[512,128]{1,0:T(8,128)(2,1)S(1)}, bf16[512,128]{1,0:T(8,128)(2,1)S(1)}, u32[]{:S(2)}, u32[]{:S(2)}) collective-permute-start(bf16[512,128]{1,0:T(8,128)(2,1)S(1)} %pad_maximum_fusion.refs_0_), channel_id=1, source_target_pairs={{0,1},{1,0},{2,3},{3,2},{4,5},{5,4},{6,7},{7,6},{8,9},{9,8},{10,11... | collective-permute-start | bytes 393224 | tf_op jit(solution)/shard_map/ppermute | solution.py:297
  27.9 0.1 copy.11
  28.1 2.3 %collective-permute-done.6.refs_1_ = bf16[512,128]{1,0:T(8,128)(2,1)S(1)} collective-permute-done((bf16[512,128]{1,0:T(8,128)(2,1)S(1)}, bf16[512,128]{1,0:T(8,128)(2,1)S(1)}, u32[]{:S(2)}, u32[]{:S(2)}) %collective-permute-start.6) | collective-permute-done | bytes 131104 | tf_op jit(solution)/shard_map/ppermute | solution.py:297
  30.4 0.1 copy.13
  30.6 1.1 %collective-permute-done.7.refs_2_ = bf16[512,128]{1,0:T(8,128)(2,1)S(1)} collective-permute-done((bf16[512,128]{1,0:T(8,128)(2,1)S(1)}, bf16[512,128]{1,0:T(8,128)(2,1)S(1)}, u32[]{:S(2)}, u32[]{:S(2)}) %collective-permute-start.7) | collective-permute-done | bytes 131104 | tf_op jit(solution)/shard_map/ppermute | solution.py:297
  31.7 0.1 copy.15
  31.8 0.1 copy.17
  32.1 0.5 %collective-permute-start.11 = (bf16[512,128]{1,0:T(8,128)(2,1)S(1)}, bf16[512,128]{1,0:T(8,128)(2,1)S(1)}, u32[]{:S(2)}, u32[]{:S(2)}) collective-permute-start(bf16[512,128]{1,0:T(8,128)(2,1)S(1)} %collective-permute-done.7.refs_2_), channel_id=1, source_target_pairs={{0,4},{4,0},{8,12},{12,8},{16,20},{20,16},{24,28},{28,24},{1,5},{5... | collective-permute-start | bytes 393224 | tf_op jit(solution)/shard_map/ppermute | solution.py:306
  32.7 0.3 fusion
  33.0 0.9 %reshape.27 = f32[16,4096]{1,0:T(8,128)} reshape(f32[16,64,64]{2,1,0:T(8,128)S(1)} %fusion) | data formatting | bytes 524288 | tf_op jit(solution)/shard_map/reshape | solution.py:332
  34.0 4.0 %gram.1 = f32[1024,512]{1,0:T(8,128)} custom-call(bf16[512,128]{1,0:T(8,128)(2,1)S(1)} %pad_maximum_fusion.refs_0_, bf16[512,128]{1,0:T(8,128)(2,1)S(1)} %collective-permute-done.6.refs_1_, bf16[512,128]{1,0:T(8,128)(2,1)S(1)} %collective-permute-done.7.refs_2_, bf16[512,128]{1,0:T(8,128)(2,1)S(1)} %collective-permute-done.8.refs_3_, ...), custom_call_target="tpu_custom_call" | custom-call | tf_op jit(solution)/shard_map/gram/pallas_call | solution.py:262
  (22 shorter events, 0.5 us)
Async XLA Ops:
  7.2 6.1 %collective-permute-start = (bf16[208,128]{1,0:T(8,128)(2,1)S(1)}, bf16[208,128]{1,0:T(8,128)(2,1)S(1)}, u32[]{:S(2)}, u32[]{:S(2)}) collective-permute-start(bf16[208,128]{1,0:T(8,128)(2,1)S(1)} %get-tuple-element.7), channel_id=1, source_target_pairs={{0,3},{1,2},{2,1},{3,0},{4,7},{5,6},{6,5},{7,4},{8,11},{9,10},{10,... | collective-permute-start | bytes 159752 | tf_op jit(solution)/shard_map/ppermute | solution.py:297
  11.2 4.1 %collective-permute-start.1 = (bf16[208,128]{1,0:T(8,128)(2,1)S(1)}, bf16[208,128]{1,0:T(8,128)(2,1)S(1)}, u32[]{:S(2)}, u32[]{:S(2)}) collective-permute-start(bf16[208,128]{1,0:T(8,128)(2,1)S(1)} %get-tuple-element.8), channel_id=1, source_target_pairs={{0,2},{1,3},{2,0},{3,1},{4,6},{5,7},{6,4},{7,5},{8,10},{9,11},{10,... | collective-permute-start | bytes 159752 | tf_op jit(solution)/shard_map/ppermute | solution.py:297
  11.7 4.1 %collective-permute-start.2 = (bf16[208,128]{1,0:T(8,128)(2,1)S(1)}, bf16[208,128]{1,0:T(8,128)(2,1)S(1)}, u32[]{:S(2)}, u32[]{:S(2)}) collective-permute-start(bf16[208,128]{1,0:T(8,128)(2,1)S(1)} %get-tuple-element.9), channel_id=1, source_target_pairs={{0,1},{1,0},{2,3},{3,2},{4,5},{5,4},{6,7},{7,6},{8,9},{9,8},{10,11... | collective-permute-start | bytes 159752 | tf_op jit(solution)/shard_map/ppermute | solution.py:297
  15.9 5.9 %collective-permute-start.3 = (bf16[128,128]{1,0:T(8,128)(2,1)S(1)}, bf16[128,128]{1,0:T(8,128)(2,1)S(1)}, u32[]{:S(2)}, u32[]{:S(2)}) collective-permute-start(bf16[128,128]{1,0:T(8,128)(2,1)S(1)} %join.1), channel_id=1, source_target_pairs={{0,24},{4,28},{8,16},{12,20},{16,8},{20,12},{24,0},{28,4},{1,25},{... | collective-permute-start | bytes 98312 | tf_op jit(solution)/shard_map/ppermute | solution.py:300
  19.5 4.8 %collective-permute-start.4 = (bf16[128,128]{1,0:T(8,128)(2,1)S(1)}, bf16[128,128]{1,0:T(8,128)(2,1)S(1)}, u32[]{:S(2)}, u32[]{:S(2)}) collective-permute-start(bf16[128,128]{1,0:T(8,128)(2,1)S(1)} %join.1), channel_id=1, source_target_pairs={{0,16},{4,20},{8,24},{12,28},{16,0},{20,4},{24,8},{28,12},{1,17},{... | collective-permute-start | bytes 98312 | tf_op jit(solution)/shard_map/ppermute | solution.py:300
  19.5 4.8 %collective-permute-start.5 = (bf16[128,128]{1,0:T(8,128)(2,1)S(1)}, bf16[128,128]{1,0:T(8,128)(2,1)S(1)}, u32[]{:S(2)}, u32[]{:S(2)}) collective-permute-start(bf16[128,128]{1,0:T(8,128)(2,1)S(1)} %join.1), channel_id=1, source_target_pairs={{0,8},{4,12},{8,0},{12,4},{16,24},{20,28},{24,16},{28,20},{1,9},{5... | collective-permute-start | bytes 98312 | tf_op jit(solution)/shard_map/ppermute | solution.py:300
  24.4 6.0 %collective-permute-start.6 = (bf16[512,128]{1,0:T(8,128)(2,1)S(1)}, bf16[512,128]{1,0:T(8,128)(2,1)S(1)}, u32[]{:S(2)}, u32[]{:S(2)}) collective-permute-start(bf16[512,128]{1,0:T(8,128)(2,1)S(1)} %pad_maximum_fusion.refs_0_), channel_id=1, source_target_pairs={{0,3},{1,2},{2,1},{3,0},{4,7},{5,6},{6,5},{7,4},{8,11},{9,10},{10,... | collective-permute-start | bytes 393224 | tf_op jit(solution)/shard_map/ppermute | solution.py:297
  25.9 5.8 %collective-permute-start.7 = (bf16[512,128]{1,0:T(8,128)(2,1)S(1)}, bf16[512,128]{1,0:T(8,128)(2,1)S(1)}, u32[]{:S(2)}, u32[]{:S(2)}) collective-permute-start(bf16[512,128]{1,0:T(8,128)(2,1)S(1)} %pad_maximum_fusion.refs_0_), channel_id=1, source_target_pairs={{0,2},{1,3},{2,0},{3,1},{4,6},{5,7},{6,4},{7,5},{8,10},{9,11},{10,... | collective-permute-start | bytes 393224 | tf_op jit(solution)/shard_map/ppermute | solution.py:297
  26.4 5.4 %collective-permute-start.8 = (bf16[512,128]{1,0:T(8,128)(2,1)S(1)}, bf16[512,128]{1,0:T(8,128)(2,1)S(1)}, u32[]{:S(2)}, u32[]{:S(2)}) collective-permute-start(bf16[512,128]{1,0:T(8,128)(2,1)S(1)} %pad_maximum_fusion.refs_0_), channel_id=1, source_target_pairs={{0,1},{1,0},{2,3},{3,2},{4,5},{5,4},{6,7},{7,6},{8,9},{9,8},{10,11... | collective-permute-start | bytes 393224 | tf_op jit(solution)/shard_map/ppermute | solution.py:297
  28.0 5.9 %collective-permute-start.9 = (bf16[512,128]{1,0:T(8,128)(2,1)S(1)}, bf16[512,128]{1,0:T(8,128)(2,1)S(1)}, u32[]{:S(2)}, u32[]{:S(2)}) collective-permute-start(bf16[512,128]{1,0:T(8,128)(2,1)S(1)} %pad_maximum_fusion.refs_0_), channel_id=1, source_target_pairs={{0,4},{4,0},{8,12},{12,8},{16,20},{20,16},{24,28},{28,24},{1,5},{5... | collective-permute-start | bytes 393224 | tf_op jit(solution)/shard_map/ppermute | solution.py:306
  32.1 1.9 %collective-permute-start.10 = (bf16[512,128]{1,0:T(8,128)(2,1)S(1)}, bf16[512,128]{1,0:T(8,128)(2,1)S(1)}, u32[]{:S(2)}, u32[]{:S(2)}) collective-permute-start(bf16[512,128]{1,0:T(8,128)(2,1)S(1)} %collective-permute-done.6.refs_1_), channel_id=1, source_target_pairs={{0,4},{4,0},{8,12},{12,8},{16,20},{20,16},{24,28},{28,24},{1,5},{5... | collective-permute-start | bytes 393224 | tf_op jit(solution)/shard_map/ppermute | solution.py:306
  32.1 1.8 %collective-permute-start.11 = (bf16[512,128]{1,0:T(8,128)(2,1)S(1)}, bf16[512,128]{1,0:T(8,128)(2,1)S(1)}, u32[]{:S(2)}, u32[]{:S(2)}) collective-permute-start(bf16[512,128]{1,0:T(8,128)(2,1)S(1)} %collective-permute-done.7.refs_2_), channel_id=1, source_target_pairs={{0,4},{4,0},{8,12},{12,8},{16,20},{20,16},{24,28},{28,24},{1,5},{5... | collective-permute-start | bytes 393224 | tf_op jit(solution)/shard_map/ppermute | solution.py:306
  32.6 1.3 %collective-permute-start.12 = (bf16[512,128]{1,0:T(8,128)(2,1)S(1)}, bf16[512,128]{1,0:T(8,128)(2,1)S(1)}, u32[]{:S(2)}, u32[]{:S(2)}) collective-permute-start(bf16[512,128]{1,0:T(8,128)(2,1)S(1)} %collective-permute-done.8.refs_3_), channel_id=1, source_target_pairs={{0,4},{4,0},{8,12},{12,8},{16,20},{20,16},{24,28},{28,24},{1,5},{5... | collective-permute-start | bytes 393224 | tf_op jit(solution)/shard_map/ppermute | solution.py:306

commit v3 on v2

--- a/solution.py
+++ b/solution.py
@@ -10,11 +10,10 @@
 SEQ = 8
 LOG2E = 1.4426950408889634
 LANES = 128
-CHUNK = 3456
+SHARES = (0.15, 0.35, 0.35, 1.0)
 SUB = 256
 STAT = 16
 AHEAD = 20
-FIRST = 1152
 F32 = jnp.float32
 BF16 = jnp.bfloat16
 
@@ -33,6 +32,16 @@
     return out
 
 
+def _plan(total):
+    out, start = [], 0
+    for share in SHARES:
+        size = min(_cdiv(int(total * share), LANES) * LANES, total - start)
+        if size > 0:
+            out.append((start, size))
+            start += size
+    return out
+
+
 def _partner(i, k, n):
     return i ^ k if n & (n - 1) == 0 else (i + k) % n
 
@@ -46,7 +55,7 @@
 ):
     outs = rest[:groups]
     buf, lab, act, pin, pext, wide, acc, plab, top, msg, sem, lsem, psem = rest[groups:]
-    chunks = _sizes(vocab, CHUNK, FIRST)
+    chunks = _plan(vocab)
     queue, loads, pout_loads = [], [], []
     label_load = pltpu.make_async_copy(labels_hbm, lab, sem.at[0])
     act_load = pltpu.make_async_copy(act_hbm, act, sem.at[1])
@@ -56,7 +65,7 @@
         loads.append(pltpu.make_async_copy(logits_hbm.at[cols, :], buf.at[cols, :], lsem.at[n]))
         pout_loads.append(pltpu.make_async_copy(pout_hbm.at[:, cols], pext.at[0:k_out, cols], psem.at[n]))
         queue.append((loads[n], pout_loads[n], label_load) if n == 0 else (loads[n], pout_loads[n]))
-        if n == min(3, len(chunks) - 1):
+        if n == min(1, len(chunks) - 1):
             queue.append((act_load, pin_load))
     started = 0
 
@@ -142,7 +151,7 @@
     k_out = pout.shape[0]
     rows = k_in + 2 * k_out + STAT
     share = tokens // groups
-    n_chunks = len(_sizes(vocab, CHUNK, FIRST))
+    n_chunks = len(_plan(vocab))
     any_spec = pl.BlockSpec(memory_space=pl.ANY)
     return pl.pallas_call(
         functools.partial(
@@ -157,7 +166,7 @@
             pltpu.VMEM((tokens, width), BF16),
             pltpu.VMEM((k_in, width), BF16),
             pltpu.VMEM((k_out + STAT, vocab), BF16),
-            pltpu.VMEM((k_out, CHUNK), F32),
+            pltpu.VMEM((k_out, max(size for _, size in _plan(vocab)) + LANES), F32),
             pltpu.VMEM((k_out + STAT, tokens), F32),
             pltpu.VMEM((k_out, tokens), F32),
             pltpu.VMEM((1, tokens), F32),
@@ -284,6 +293,39 @@
     )(*_on_chip(ins))
 
 
+def _features_kernel(*refs, examples, own, k_in, k_out):
+    ins, out, turned = refs[:-2], refs[-2], refs[-1]
+    rows = k_in + k_out
+    first = lax.axis_index("fsdp") * own
+    parts = []
+    for k, src in enumerate(ins):
+        turned[k] = jnp.transpose(src[0:rows, :].astype(F32))
+        for s in range(LANES // examples):
+            parts.append(turned[k, pl.ds(pl.multiple_of(s * examples + first, 8), own), :])
+    left = jnp.concatenate([p[:, :k_in] for p in parts], axis=0).astype(BF16)
+    rights = [jnp.concatenate([p[:, k_in:], p[:, k_in:]], axis=1) for p in parts]
+    width = 4 * LANES
+    for n in range(0, k_in * k_out, width):
+        row = lax.broadcasted_iota(jnp.int32, (k_in, width), 0)
+        col = lax.broadcasted_iota(jnp.int32, (k_in, width), 1) + n
+        spread = jnp.where((col >= row * k_out) & (col < (row + 1) * k_out), 1.0, 0.0).astype(BF16)
+        wide = jnp.dot(left, spread, preferred_element_type=F32)
+        for c in range(0, width, LANES):
+            terms = [wide[t * own : (t + 1) * own, c : c + LANES] * r for t, r in enumerate(rights)]
+            out[:, n + c : n + c + LANES] = functools.reduce(jnp.add, terms)
+
+
+def _features(arrays, examples, own, k_in, k_out):
+    return pl.pallas_call(
+        functools.partial(_features_kernel, examples=examples, own=own, k_in=k_in, k_out=k_out),
+        out_shape=pltpu.VMEM((own, k_in * k_out), F32),
+        in_specs=[pl.BlockSpec(memory_space=pltpu.VMEM)] * len(arrays),
+        out_specs=pl.BlockSpec(memory_space=pltpu.VMEM),
+        scratch_shapes=[pltpu.VMEM((len(arrays), LANES, k_in + k_out), F32)],
+        name="own_features",
+    )(*_on_chip(arrays))
+
+
 def body(logits, labels, activations, proj_in, proj_out):
     n_f, n_d = lax.axis_size("fsdp"), lax.axis_size("dp")
     tokens = logits.shape[0]
@@ -314,7 +356,10 @@
     other = [other_core(a) for a in own]
 
     mine = lax.axis_index("fsdp")
-    if share >= examples:
+    group = None
+    if share == LANES and 2 * k_out == LANES and k_in == k_out and own_examples % 8 == 0 and share % examples == 0:
+        features = _features(own, examples, own_examples, k_in, k_out)
+    elif share >= examples:
         slots = share // examples
         pieces = []
         for a in own:
@@ -328,8 +373,9 @@
             whole = lax.dynamic_update_slice(whole, a[:rows][None], (order[k], 0, 0))
         whole = whole.transpose(1, 0, 2).reshape(rows, SEQ, examples)
         group = lax.dynamic_slice_in_dim(whole, mine * own_examples, own_examples, 2)
-    features = jnp.einsum("ite,jte->eij", group[:k_in], group[k_in:], preferred_element_type=F32)
-    features = features.reshape(own_examples, k_in * k_out)
+    if group is not None:
+        features = jnp.einsum("ite,jte->eij", group[:k_in], group[k_in:], preferred_element_type=F32)
+        features = features.reshape(own_examples, k_in * k_out)
 
     n_row, n_col = k_in // n_f, k_in // n_d
     lanes = examples * n_d

time: 38.1 us -> 37.4 us (0.982)
  local copies, waits for them, and re-layouts: 1.4 us -> 0.71 us
  waiting for transfers between devices: 11.5 us -> 11.9 us
    reshape x1 -> x0, local copies, waits for them, and re-layouts: 0.89 us -> none  [body(): features = features.reshape(own_examples, k_in * k_out)]
    unnamed x4 -> x1, local copies, waits for them, and re-layouts: 0.03 us -> 0.71 us
    pallas_call x0 -> x1, Pallas kernels: none -> 0.53 us  [_features(): pl.pallas_call(functools.partial(_features_kernel, examples=examples, own...]
    ppermute x6, waiting for transfers between devices: 7.42 us -> 7.88 us  [along_f(): lax.ppermute(a, 'fsdp', [(i, _partner(i, k, n_f)) for i in range(n_f)])]
  transfers between devices with their start and end apart: 13 -> 13, of which waited for: 8 -> 8; matrix products, arithmetic and copies ran while one was open for 5% -> 2% of each run, Pallas kernels for 0% -> 1%
where the time goes in v3:
time: 37.4 us; the launch traced here: 37.3 us
  starting transfers between devices  13.1 us (35%)
  waiting for transfers between devices  11.9 us (32%)
  Pallas kernels  10.9 us (29%)
  local copies, waits for them, and re-layouts  0.71 us (2%)
  between operations  0.68 us (2%)
    ppermute x6, starting transfers between devices, along_f(): lax.ppermute(a, 'fsdp', [(i, _partner(i, k, n_f)) for i in range(n_f)])  8.18 us
    ppermute x6, waiting for transfers between devices, along_f(): lax.ppermute(a, 'fsdp', [(i, _partner(i, k, n_f)) for i in range(n_f)])  7.88 us
    pallas_call x1, Pallas kernels, _local(): pl.pallas_call(functools.partial(_local_kernel, groups=groups, vocab=voca...  6.33 us
    ppermute x3, starting transfers between devices, along_z(): lax.ppermute(a, 'dp', [(i, 2 * _partner(i // 2, k, n_d // 2) + i % 2) for...  4.45 us
    ppermute x3, waiting for transfers between devices, along_z(): lax.ppermute(a, 'dp', [(i, 2 * _partner(i // 2, k, n_d // 2) + i % 2) for...  4.03 us
    pallas_call x1, Pallas kernels, _gram(): pl.pallas_call(functools.partial(_gram_kernel, n_in=len(ins), blocks=bloc...  4.01 us
  transfers between devices with their start and end apart: 13, of which 8 were waited for; matrix products, arithmetic and copies ran while one was open for 2% of the time, Pallas kernels for 1%

profile of v3, /device:TPU:0, one launch (start us, length us, event | category | flops | bytes accessed | tf_op | source)
XLA Modules:
  0.0 37.3 jit_solution(10795313866256228809)
XLA Ops:
  0.6 6.3 %local_pass.1 = (bf16[208,128]{1,0:T(8,128)(2,1)S(1)}, bf16[208,128]{1,0:T(8,128)(2,1)S(1)}, bf16[208,128]{1,0:T(8,128)(2,1)S(1)}, bf16[208,128]{1,0:T(8,128)(2,1)S(1)}) custom-call(bf16[8000,512]{1,0:T(8,128)(2,1)} %bitcast.4, s32[1,512]{1,0:T(1,128)} %bitcast.7, bf16[512,1280]{1,0:T(8,128)(2,1)} %act_hbm.1, bf16[64,1280]{1,0:T(8,128)(2,1)} %bitcast.6, ...), custom_call_target="tpu_custom_call" | custom-call | tf_op jit(solution)/shard_map/local_pass/pallas_call | solution.py:156
  7.0 4.0 %collective-permute-start = (bf16[208,128]{1,0:T(8,128)(2,1)S(1)}, bf16[208,128]{1,0:T(8,128)(2,1)S(1)}, u32[]{:S(2)}, u32[]{:S(2)}) collective-permute-start(bf16[208,128]{1,0:T(8,128)(2,1)S(1)} %get-tuple-element.7), channel_id=1, source_target_pairs={{0,3},{1,2},{2,1},{3,0},{4,7},{5,6},{6,5},{7,4},{8,11},{9,10},{10,... | collective-permute-start | bytes 159752 | tf_op jit(solution)/shard_map/ppermute | solution.py:339
  11.0 0.5 %collective-permute-start.1 = (bf16[208,128]{1,0:T(8,128)(2,1)S(1)}, bf16[208,128]{1,0:T(8,128)(2,1)S(1)}, u32[]{:S(2)}, u32[]{:S(2)}) collective-permute-start(bf16[208,128]{1,0:T(8,128)(2,1)S(1)} %get-tuple-element.8), channel_id=1, source_target_pairs={{0,2},{1,3},{2,0},{3,1},{4,6},{5,7},{6,4},{7,5},{8,10},{9,11},{10,... | collective-permute-start | bytes 159752 | tf_op jit(solution)/shard_map/ppermute | solution.py:339
  11.5 0.1 collective-permute-start.2
  11.6 1.5 %collective-permute-done.refs_1_ = bf16[208,128]{1,0:T(8,128)(2,1)S(1)} collective-permute-done((bf16[208,128]{1,0:T(8,128)(2,1)S(1)}, bf16[208,128]{1,0:T(8,128)(2,1)S(1)}, u32[]{:S(2)}, u32[]{:S(2)}) %collective-permute-start) | collective-permute-done | bytes 53280 | tf_op jit(solution)/shard_map/ppermute | solution.py:339
  13.1 2.0 %collective-permute-done.1.refs_2_ = bf16[208,128]{1,0:T(8,128)(2,1)S(1)} collective-permute-done((bf16[208,128]{1,0:T(8,128)(2,1)S(1)}, bf16[208,128]{1,0:T(8,128)(2,1)S(1)}, u32[]{:S(2)}, u32[]{:S(2)}) %collective-permute-start.1) | collective-permute-done | bytes 53280 | tf_op jit(solution)/shard_map/ppermute | solution.py:339
  15.1 0.5 %collective-permute-done.2.refs_3_ = bf16[208,128]{1,0:T(8,128)(2,1)S(1)} collective-permute-done((bf16[208,128]{1,0:T(8,128)(2,1)S(1)}, bf16[208,128]{1,0:T(8,128)(2,1)S(1)}, u32[]{:S(2)}, u32[]{:S(2)}) %collective-permute-start.2) | collective-permute-done | bytes 53280 | tf_op jit(solution)/shard_map/ppermute | solution.py:339
  15.6 3.7 %collective-permute-start.3 = (bf16[128,128]{1,0:T(8,128)(2,1)S(1)}, bf16[128,128]{1,0:T(8,128)(2,1)S(1)}, u32[]{:S(2)}, u32[]{:S(2)}) collective-permute-start(bf16[128,128]{1,0:T(8,128)(2,1)S(1)} %join.1), channel_id=1, source_target_pairs={{0,24},{4,28},{8,16},{12,20},{16,8},{20,12},{24,0},{28,4},{1,25},{... | collective-permute-start | bytes 98312 | tf_op jit(solution)/shard_map/ppermute | solution.py:342
  19.3 0.0 collective-permute-start.4
  19.3 0.8 %collective-permute-start.5 = (bf16[128,128]{1,0:T(8,128)(2,1)S(1)}, bf16[128,128]{1,0:T(8,128)(2,1)S(1)}, u32[]{:S(2)}, u32[]{:S(2)}) collective-permute-start(bf16[128,128]{1,0:T(8,128)(2,1)S(1)} %join.1), channel_id=1, source_target_pairs={{0,8},{4,12},{8,0},{12,4},{16,24},{20,28},{24,16},{28,20},{1,9},{5... | collective-permute-start | bytes 98312 | tf_op jit(solution)/shard_map/ppermute | solution.py:342
  20.1 1.4 %collective-permute-done.3 = bf16[128,128]{1,0:T(8,128)(2,1)S(1)} collective-permute-done((bf16[128,128]{1,0:T(8,128)(2,1)S(1)}, bf16[128,128]{1,0:T(8,128)(2,1)S(1)}, u32[]{:S(2)}, u32[]{:S(2)}) %collective-permute-start.3) | collective-permute-done | bytes 32800 | tf_op jit(solution)/shard_map/ppermute | solution.py:342
  21.5 2.6 %collective-permute-done.4 = bf16[128,128]{1,0:T(8,128)(2,1)S(1)} collective-permute-done((bf16[128,128]{1,0:T(8,128)(2,1)S(1)}, bf16[128,128]{1,0:T(8,128)(2,1)S(1)}, u32[]{:S(2)}, u32[]{:S(2)}) %collective-permute-start.4) | collective-permute-done | bytes 32800 | tf_op jit(solution)/shard_map/ppermute | solution.py:342
  24.1 1.6 %collective-permute-start.6 = (bf16[512,128]{1,0:T(8,128)(2,1)S(1)}, bf16[512,128]{1,0:T(8,128)(2,1)S(1)}, u32[]{:S(2)}, u32[]{:S(2)}) collective-permute-start(bf16[512,128]{1,0:T(8,128)(2,1)S(1)} %pad_maximum_fusion.refs_0_), channel_id=1, source_target_pairs={{0,3},{1,2},{2,1},{3,0},{4,7},{5,6},{6,5},{7,4},{8,11},{9,10},{10,... | collective-permute-start | bytes 393224 | tf_op jit(solution)/shard_map/ppermute | solution.py:339
  25.7 0.5 %collective-permute-start.7 = (bf16[512,128]{1,0:T(8,128)(2,1)S(1)}, bf16[512,128]{1,0:T(8,128)(2,1)S(1)}, u32[]{:S(2)}, u32[]{:S(2)}) collective-permute-start(bf16[512,128]{1,0:T(8,128)(2,1)S(1)} %pad_maximum_fusion.refs_0_), channel_id=1, source_target_pairs={{0,2},{1,3},{2,0},{3,1},{4,6},{5,7},{6,4},{7,5},{8,10},{9,11},{10,... | collective-permute-start | bytes 393224 | tf_op jit(solution)/shard_map/ppermute | solution.py:339
  26.2 1.5 %collective-permute-start.8 = (bf16[512,128]{1,0:T(8,128)(2,1)S(1)}, bf16[512,128]{1,0:T(8,128)(2,1)S(1)}, u32[]{:S(2)}, u32[]{:S(2)}) collective-permute-start(bf16[512,128]{1,0:T(8,128)(2,1)S(1)} %pad_maximum_fusion.refs_0_), channel_id=1, source_target_pairs={{0,1},{1,0},{2,3},{3,2},{4,5},{5,4},{6,7},{7,6},{8,9},{9,8},{10,11... | collective-permute-start | bytes 393224 | tf_op jit(solution)/shard_map/ppermute | solution.py:339
  27.7 0.0 collective-permute-start.9
  27.7 2.5 %collective-permute-done.6.refs_1_ = bf16[512,128]{1,0:T(8,128)(2,1)S(1)} collective-permute-done((bf16[512,128]{1,0:T(8,128)(2,1)S(1)}, bf16[512,128]{1,0:T(8,128)(2,1)S(1)}, u32[]{:S(2)}, u32[]{:S(2)}) %collective-permute-start.6) | collective-permute-done | bytes 131104 | tf_op jit(solution)/shard_map/ppermute | solution.py:339
  30.2 0.0 collective-permute-start.10
  30.2 1.3 %collective-permute-done.7.refs_2_ = bf16[512,128]{1,0:T(8,128)(2,1)S(1)} collective-permute-done((bf16[512,128]{1,0:T(8,128)(2,1)S(1)}, bf16[512,128]{1,0:T(8,128)(2,1)S(1)}, u32[]{:S(2)}, u32[]{:S(2)}) %collective-permute-start.7) | collective-permute-done | bytes 131104 | tf_op jit(solution)/shard_map/ppermute | solution.py:339
  31.5 0.1 collective-permute-done.8.refs_3_
  31.6 0.4 %collective-permute-start.12 = (bf16[512,128]{1,0:T(8,128)(2,1)S(1)}, bf16[512,128]{1,0:T(8,128)(2,1)S(1)}, u32[]{:S(2)}, u32[]{:S(2)}) collective-permute-start(bf16[512,128]{1,0:T(8,128)(2,1)S(1)} %collective-permute-done.8.refs_3_), channel_id=1, source_target_pairs={{0,4},{4,0},{8,12},{12,8},{16,20},{20,16},{24,28},{28,24},{1,5},{5... | collective-permute-start | bytes 393224 | tf_op jit(solution)/shard_map/ppermute | solution.py:348
  32.0 0.5 %own_features.1 = f32[16,4096]{1,0:T(8,128)S(1)} custom-call(bf16[512,128]{1,0:T(8,128)(2,1)S(1)} %pad_maximum_fusion.refs_0_, bf16[512,128]{1,0:T(8,128)(2,1)S(1)} %collective-permute-done.6.refs_1_, bf16[512,128]{1,0:T(8,128)(2,1)S(1)} %collective-permute-done.7.refs_2_, bf16[512,128]{1,0:T(8,128)(2,1)S(1)} %collective-permute-done.8.refs_3_), custom_call_target="tpu_custom_call" | custom-call | tf_op jit(solution)/shard_map/own_features/pallas_call | solution.py:319
  32.5 0.7 %copy.7 = f32[16,4096]{1,0:T(8,128)} copy(f32[16,4096]{1,0:T(8,128)S(1)} %own_features.1) | data formatting | bytes 524288
  33.3 4.0 %gram.1 = f32[1024,512]{1,0:T(8,128)} custom-call(bf16[512,128]{1,0:T(8,128)(2,1)S(1)} %pad_maximum_fusion.refs_0_, bf16[512,128]{1,0:T(8,128)(2,1)S(1)} %collective-permute-done.6.refs_1_, bf16[512,128]{1,0:T(8,128)(2,1)S(1)} %collective-permute-done.7.refs_2_, bf16[512,128]{1,0:T(8,128)(2,1)S(1)} %collective-permute-done.8.refs_3_, ...), custom_call_target="tpu_custom_call" | custom-call | tf_op jit(solution)/shard_map/gram/pallas_call | solution.py:271
  (8 shorter events, 0.1 us)
Async XLA Ops:
  7.0 6.1 %collective-permute-start = (bf16[208,128]{1,0:T(8,128)(2,1)S(1)}, bf16[208,128]{1,0:T(8,128)(2,1)S(1)}, u32[]{:S(2)}, u32[]{:S(2)}) collective-permute-start(bf16[208,128]{1,0:T(8,128)(2,1)S(1)} %get-tuple-element.7), channel_id=1, source_target_pairs={{0,3},{1,2},{2,1},{3,0},{4,7},{5,6},{6,5},{7,4},{8,11},{9,10},{10,... | collective-permute-start | bytes 159752 | tf_op jit(solution)/shard_map/ppermute | solution.py:339
  11.0 4.1 %collective-permute-start.1 = (bf16[208,128]{1,0:T(8,128)(2,1)S(1)}, bf16[208,128]{1,0:T(8,128)(2,1)S(1)}, u32[]{:S(2)}, u32[]{:S(2)}) collective-permute-start(bf16[208,128]{1,0:T(8,128)(2,1)S(1)} %get-tuple-element.8), channel_id=1, source_target_pairs={{0,2},{1,3},{2,0},{3,1},{4,6},{5,7},{6,4},{7,5},{8,10},{9,11},{10,... | collective-permute-start | bytes 159752 | tf_op jit(solution)/shard_map/ppermute | solution.py:339
  11.5 4.1 %collective-permute-start.2 = (bf16[208,128]{1,0:T(8,128)(2,1)S(1)}, bf16[208,128]{1,0:T(8,128)(2,1)S(1)}, u32[]{:S(2)}, u32[]{:S(2)}) collective-permute-start(bf16[208,128]{1,0:T(8,128)(2,1)S(1)} %get-tuple-element.9), channel_id=1, source_target_pairs={{0,1},{1,0},{2,3},{3,2},{4,5},{5,4},{6,7},{7,6},{8,9},{9,8},{10,11... | collective-permute-start | bytes 159752 | tf_op jit(solution)/shard_map/ppermute | solution.py:339
  15.6 5.9 %collective-permute-start.3 = (bf16[128,128]{1,0:T(8,128)(2,1)S(1)}, bf16[128,128]{1,0:T(8,128)(2,1)S(1)}, u32[]{:S(2)}, u32[]{:S(2)}) collective-permute-start(bf16[128,128]{1,0:T(8,128)(2,1)S(1)} %join.1), channel_id=1, source_target_pairs={{0,24},{4,28},{8,16},{12,20},{16,8},{20,12},{24,0},{28,4},{1,25},{... | collective-permute-start | bytes 98312 | tf_op jit(solution)/shard_map/ppermute | solution.py:342
  19.3 4.8 %collective-permute-start.4 = (bf16[128,128]{1,0:T(8,128)(2,1)S(1)}, bf16[128,128]{1,0:T(8,128)(2,1)S(1)}, u32[]{:S(2)}, u32[]{:S(2)}) collective-permute-start(bf16[128,128]{1,0:T(8,128)(2,1)S(1)} %join.1), channel_id=1, source_target_pairs={{0,16},{4,20},{8,24},{12,28},{16,0},{20,4},{24,8},{28,12},{1,17},{... | collective-permute-start | bytes 98312 | tf_op jit(solution)/shard_map/ppermute | solution.py:342
  19.3 4.8 %collective-permute-start.5 = (bf16[128,128]{1,0:T(8,128)(2,1)S(1)}, bf16[128,128]{1,0:T(8,128)(2,1)S(1)}, u32[]{:S(2)}, u32[]{:S(2)}) collective-permute-start(bf16[128,128]{1,0:T(8,128)(2,1)S(1)} %join.1), channel_id=1, source_target_pairs={{0,8},{4,12},{8,0},{12,4},{16,24},{20,28},{24,16},{28,20},{1,9},{5... | collective-permute-start | bytes 98312 | tf_op jit(solution)/shard_map/ppermute | solution.py:342
  24.1 6.0 %collective-permute-start.6 = (bf16[512,128]{1,0:T(8,128)(2,1)S(1)}, bf16[512,128]{1,0:T(8,128)(2,1)S(1)}, u32[]{:S(2)}, u32[]{:S(2)}) collective-permute-start(bf16[512,128]{1,0:T(8,128)(2,1)S(1)} %pad_maximum_fusion.refs_0_), channel_id=1, source_target_pairs={{0,3},{1,2},{2,1},{3,0},{4,7},{5,6},{6,5},{7,4},{8,11},{9,10},{10,... | collective-permute-start | bytes 393224 | tf_op jit(solution)/shard_map/ppermute | solution.py:339
  25.7 5.8 %collective-permute-start.7 = (bf16[512,128]{1,0:T(8,128)(2,1)S(1)}, bf16[512,128]{1,0:T(8,128)(2,1)S(1)}, u32[]{:S(2)}, u32[]{:S(2)}) collective-permute-start(bf16[512,128]{1,0:T(8,128)(2,1)S(1)} %pad_maximum_fusion.refs_0_), channel_id=1, source_target_pairs={{0,2},{1,3},{2,0},{3,1},{4,6},{5,7},{6,4},{7,5},{8,10},{9,11},{10,... | collective-permute-start | bytes 393224 | tf_op jit(solution)/shard_map/ppermute | solution.py:339
  26.2 5.4 %collective-permute-start.8 = (bf16[512,128]{1,0:T(8,128)(2,1)S(1)}, bf16[512,128]{1,0:T(8,128)(2,1)S(1)}, u32[]{:S(2)}, u32[]{:S(2)}) collective-permute-start(bf16[512,128]{1,0:T(8,128)(2,1)S(1)} %pad_maximum_fusion.refs_0_), channel_id=1, source_target_pairs={{0,1},{1,0},{2,3},{3,2},{4,5},{5,4},{6,7},{7,6},{8,9},{9,8},{10,11... | collective-permute-start | bytes 393224 | tf_op jit(solution)/shard_map/ppermute | solution.py:339
  27.7 5.5 %collective-permute-start.9 = (bf16[512,128]{1,0:T(8,128)(2,1)S(1)}, bf16[512,128]{1,0:T(8,128)(2,1)S(1)}, u32[]{:S(2)}, u32[]{:S(2)}) collective-permute-start(bf16[512,128]{1,0:T(8,128)(2,1)S(1)} %pad_maximum_fusion.refs_0_), channel_id=1, source_target_pairs={{0,4},{4,0},{8,12},{12,8},{16,20},{20,16},{24,28},{28,24},{1,5},{5... | collective-permute-start | bytes 393224 | tf_op jit(solution)/shard_map/ppermute | solution.py:348
  30.2 3.1 %collective-permute-start.10 = (bf16[512,128]{1,0:T(8,128)(2,1)S(1)}, bf16[512,128]{1,0:T(8,128)(2,1)S(1)}, u32[]{:S(2)}, u32[]{:S(2)}) collective-permute-start(bf16[512,128]{1,0:T(8,128)(2,1)S(1)} %collective-permute-done.6.refs_1_), channel_id=1, source_target_pairs={{0,4},{4,0},{8,12},{12,8},{16,20},{20,16},{24,28},{28,24},{1,5},{5... | collective-permute-start | bytes 393224 | tf_op jit(solution)/shard_map/ppermute | solution.py:348
  31.5 1.8 %collective-permute-start.11 = (bf16[512,128]{1,0:T(8,128)(2,1)S(1)}, bf16[512,128]{1,0:T(8,128)(2,1)S(1)}, u32[]{:S(2)}, u32[]{:S(2)}) collective-permute-start(bf16[512,128]{1,0:T(8,128)(2,1)S(1)} %collective-permute-done.7.refs_2_), channel_id=1, source_target_pairs={{0,4},{4,0},{8,12},{12,8},{16,20},{20,16},{24,28},{28,24},{1,5},{5... | collective-permute-start | bytes 393224 | tf_op jit(solution)/shard_map/ppermute | solution.py:348
  31.6 1.7 %collective-permute-start.12 = (bf16[512,128]{1,0:T(8,128)(2,1)S(1)}, bf16[512,128]{1,0:T(8,128)(2,1)S(1)}, u32[]{:S(2)}, u32[]{:S(2)}) collective-permute-start(bf16[512,128]{1,0:T(8,128)(2,1)S(1)} %collective-permute-done.8.refs_3_), channel_id=1, source_target_pairs={{0,4},{4,0},{8,12},{12,8},{16,20},{20,16},{24,28},{28,24},{1,5},{5... | collective-permute-start | bytes 393224 | tf_op jit(solution)/shard_map/ppermute | solution.py:348

commit v4 on v3

--- a/solution.py
+++ b/solution.py
@@ -13,6 +13,7 @@
 SHARES = (0.15, 0.35, 0.35, 1.0)
 SUB = 256
 STAT = 16
+GROUPS = 4
 AHEAD = 20
 F32 = jnp.float32
 BF16 = jnp.bfloat16
@@ -222,7 +223,7 @@
                     dest[at : at + 16, cols] = total.astype(BF16)
 
     feature_rows(n_row, n_col, fcol, 0)
-    step = max(1, n_row // 4)
+    step = max(1, n_row // GROUPS)
     copies = []
     for b, i in enumerate(range(0, n_row, step)):
         feature_rows(i, step, frow, i * k_out)
@@ -238,9 +239,11 @@
 
 
 def _gram_kernel(*refs, n_in, blocks, examples, n_row, n_col, k_in, k_out):
-    ins, out_hbm = refs[:n_in], refs[n_in]
-    x, frow, fcol, res, sem = refs[n_in + 1 :]
+    ins, feats = refs[:n_in], refs[n_in]
+    out_hbm, feats_hbm, x, frow, fcol, res, sem = refs[n_in + 1 :]
     rows = k_in + k_out
+    leave = pltpu.make_async_copy(feats, feats_hbm, sem.at[sem.shape[0] - 1])
+    leave.start()
     half = n_in // 2
     if blocks:
         row_first = lax.axis_index("fsdp") * n_row
@@ -264,9 +267,10 @@
     else:
         x[...] = ins[0][...].astype(F32)
     _gram_body(x, out_hbm, frow, fcol, res, sem, n_row, n_col, k_out)
-
-
-def _gram(ins, blocks, examples, lanes, n_row, n_col, k_in, k_out):
+    leave.wait()
+
+
+def _gram(ins, feats, blocks, examples, lanes, n_row, n_col, k_in, k_out):
     rows, cols = n_row * k_out, n_col * k_out
     return pl.pallas_call(
         functools.partial(
@@ -279,18 +283,18 @@
             k_in=k_in,
             k_out=k_out,
         ),
-        out_shape=jax.ShapeDtypeStruct((rows, cols), F32),
-        in_specs=[pl.BlockSpec(memory_space=pltpu.VMEM)] * len(ins),
-        out_specs=pl.BlockSpec(memory_space=pl.ANY),
+        out_shape=[jax.ShapeDtypeStruct((rows, cols), F32), jax.ShapeDtypeStruct(feats.shape, F32)],
+        in_specs=[pl.BlockSpec(memory_space=pltpu.VMEM)] * (len(ins) + 1),
+        out_specs=[pl.BlockSpec(memory_space=pltpu.HBM)] * 2,
         scratch_shapes=[
             pltpu.VMEM((SEQ, n_row + n_col + k_out, lanes), F32),
             pltpu.VMEM((rows, lanes), BF16),
             pltpu.VMEM((cols, lanes), BF16),
             pltpu.VMEM((rows, cols), F32),
-            pltpu.SemaphoreType.DMA((8,)),
+            pltpu.SemaphoreType.DMA((GROUPS + 1,)),
         ],
         name="gram",
-    )(*_on_chip(ins))
+    )(*_on_chip(ins + [feats]))
 
 
 def _features_kernel(*refs, examples, own, k_in, k_out):
@@ -351,8 +355,8 @@
     parts = [parts[0]] + [along_f(parts[k], k) for k in far_first(n_f)]
     joined = _join(parts, k_in, k_out)
     n_z = n_d // 2
-    column = jnp.concatenate([joined] + [along_z(joined, k) for k in far_first(n_z)], axis=0)
-    own = [column] + [along_f(column, k) for k in far_first(n_f)]
+    column = jnp.concatenate([joined] + [along_z(joined, k) for k in range(1, n_z)], axis=0)
+    own = [column] + [along_f(column, k) for k in range(1, n_f)]
     other = [other_core(a) for a in own]
 
     mine = lax.axis_index("fsdp")
@@ -367,7 +371,7 @@
             pieces.append(lax.dynamic_slice_in_dim(part, mine * own_examples, own_examples, 2))
         group = jnp.concatenate(pieces, axis=1)
     else:
-        order = [mine] + [_partner(mine, k, n_f) if n_f & (n_f - 1) == 0 else (mine - k) % n_f for k in far_first(n_f)]
+        order = [mine] + [_partner(mine, k, n_f) if n_f & (n_f - 1) == 0 else (mine - k) % n_f for k in range(1, n_f)]
         whole = jnp.zeros((n_f, rows, share), BF16)
         for k, a in enumerate(own):
             whole = lax.dynamic_update_slice(whole, a[:rows][None], (order[k], 0, 0))
@@ -380,9 +384,9 @@
     n_row, n_col = k_in // n_f, k_in // n_d
     lanes = examples * n_d
     if share == LANES and 2 * examples == LANES and n_row % 8 == 0 and n_col % 8 == 0:
-        gram = _gram(own + other, n_z, examples, lanes, n_row, n_col, k_in, k_out)
+        gram, features = _gram(own + other, features, n_z, examples, lanes, n_row, n_col, k_in, k_out)
     else:
-        order = [mine] + [_partner(mine, k, n_f) if n_f & (n_f - 1) == 0 else (mine - k) % n_f for k in far_first(n_f)]
+        order = [mine] + [_partner(mine, k, n_f) if n_f & (n_f - 1) == 0 else (mine - k) % n_f for k in range(1, n_f)]
         whole = jnp.zeros((n_f, 2, n_z, rows, share), BF16)
         for c, arrays in enumerate((own, other)):
             for k, a in enumerate(arrays):
@@ -397,7 +401,7 @@
             ],
             axis=1,
         )
-        gram = _gram([whole], 0, examples, lanes, n_row, n_col, k_in, k_out)
+        gram, features = _gram([whole], features, 0, examples, lanes, n_row, n_col, k_in, k_out)
     return features, gram
 
 

time: 37.4 us -> 37.1 us (level)
  local copies, waits for them, and re-layouts: 0.71 us -> 0 us
  waiting for transfers between devices: 11.9 us -> 12.4 us
    unnamed x1 -> x0, local copies, waits for them, and re-layouts: 0.71 us -> none
    ppermute x4, waiting for transfers between devices: 0.01 us -> 0.46 us  [other_core(): return lax.ppermute(a, 'dp', [(i, i ^ 1) for i in range(n_d)])]
  transfers between devices with their start and end apart: 13 -> 13, of which waited for: 8 -> 10; matrix products, arithmetic and copies ran while one was open for 2% -> 0% of each run, Pallas kernels for 1% -> 1%
where the time goes in v4:
time: 37.1 us; the launch traced here: 37 us
  starting transfers between devices  13.1 us (35%)
  waiting for transfers between devices  12.4 us (33%)
  Pallas kernels  10.9 us (29%)
  between operations  0.68 us (2%)
    ppermute x6, starting transfers between devices, along_f(): lax.ppermute(a, 'fsdp', [(i, _partner(i, k, n_f)) for i in range(n_f)])  8.18 us
    ppermute x6, waiting for transfers between devices, along_f(): lax.ppermute(a, 'fsdp', [(i, _partner(i, k, n_f)) for i in range(n_f)])  7.88 us
    pallas_call x1, Pallas kernels, _local(): pl.pallas_call(functools.partial(_local_kernel, groups=groups, vocab=voca...  6.33 us
    ppermute x3, starting transfers between devices, along_z(): lax.ppermute(a, 'dp', [(i, 2 * _partner(i // 2, k, n_d // 2) + i % 2) for...  4.45 us
    ppermute x3, waiting for transfers between devices, along_z(): lax.ppermute(a, 'dp', [(i, 2 * _partner(i // 2, k, n_d // 2) + i % 2) for...  4.03 us
    pallas_call x1, Pallas kernels, _gram(): pl.pallas_call(functools.partial(_gram_kernel, n_in=len(ins), blocks=bloc...  3.98 us
  transfers between devices with their start and end apart: 13, of which 10 were waited for; matrix products, arithmetic and copies ran while one was open for 0% of the time, Pallas kernels for 1%

profile of v4, /device:TPU:0, one launch (start us, length us, event | category | flops | bytes accessed | tf_op | source)
XLA Modules:
  0.0 37.0 jit_solution(8806177381445081320)
XLA Ops:
  0.6 6.3 %local_pass.1 = (bf16[208,128]{1,0:T(8,128)(2,1)S(1)}, bf16[208,128]{1,0:T(8,128)(2,1)S(1)}, bf16[208,128]{1,0:T(8,128)(2,1)S(1)}, bf16[208,128]{1,0:T(8,128)(2,1)S(1)}) custom-call(bf16[8000,512]{1,0:T(8,128)(2,1)} %bitcast.4, s32[1,512]{1,0:T(1,128)} %bitcast.7, bf16[512,1280]{1,0:T(8,128)(2,1)} %act_hbm.1, bf16[64,1280]{1,0:T(8,128)(2,1)} %bitcast.6, ...), custom_call_target="tpu_custom_call" | custom-call | tf_op jit(solution)/shard_map/local_pass/pallas_call | solution.py:157
  7.0 4.0 %collective-permute-start = (bf16[208,128]{1,0:T(8,128)(2,1)S(1)}, bf16[208,128]{1,0:T(8,128)(2,1)S(1)}, u32[]{:S(2)}, u32[]{:S(2)}) collective-permute-start(bf16[208,128]{1,0:T(8,128)(2,1)S(1)} %get-tuple-element.9), channel_id=1, source_target_pairs={{0,3},{1,2},{2,1},{3,0},{4,7},{5,6},{6,5},{7,4},{8,11},{9,10},{10,... | collective-permute-start | bytes 159752 | tf_op jit(solution)/shard_map/ppermute | solution.py:343
  11.0 0.5 %collective-permute-start.1 = (bf16[208,128]{1,0:T(8,128)(2,1)S(1)}, bf16[208,128]{1,0:T(8,128)(2,1)S(1)}, u32[]{:S(2)}, u32[]{:S(2)}) collective-permute-start(bf16[208,128]{1,0:T(8,128)(2,1)S(1)} %get-tuple-element.10), channel_id=1, source_target_pairs={{0,2},{1,3},{2,0},{3,1},{4,6},{5,7},{6,4},{7,5},{8,10},{9,11},{10,... | collective-permute-start | bytes 159752 | tf_op jit(solution)/shard_map/ppermute | solution.py:343
  11.5 0.1 collective-permute-start.2
  11.6 1.5 %collective-permute-done.refs_1_ = bf16[208,128]{1,0:T(8,128)(2,1)S(1)} collective-permute-done((bf16[208,128]{1,0:T(8,128)(2,1)S(1)}, bf16[208,128]{1,0:T(8,128)(2,1)S(1)}, u32[]{:S(2)}, u32[]{:S(2)}) %collective-permute-start) | collective-permute-done | bytes 53280 | tf_op jit(solution)/shard_map/ppermute | solution.py:343
  13.1 2.0 %collective-permute-done.1.refs_2_ = bf16[208,128]{1,0:T(8,128)(2,1)S(1)} collective-permute-done((bf16[208,128]{1,0:T(8,128)(2,1)S(1)}, bf16[208,128]{1,0:T(8,128)(2,1)S(1)}, u32[]{:S(2)}, u32[]{:S(2)}) %collective-permute-start.1) | collective-permute-done | bytes 53280 | tf_op jit(solution)/shard_map/ppermute | solution.py:343
  15.1 0.5 %collective-permute-done.2.refs_3_ = bf16[208,128]{1,0:T(8,128)(2,1)S(1)} collective-permute-done((bf16[208,128]{1,0:T(8,128)(2,1)S(1)}, bf16[208,128]{1,0:T(8,128)(2,1)S(1)}, u32[]{:S(2)}, u32[]{:S(2)}) %collective-permute-start.2) | collective-permute-done | bytes 53280 | tf_op jit(solution)/shard_map/ppermute | solution.py:343
  15.6 3.7 %collective-permute-start.5 = (bf16[128,128]{1,0:T(8,128)(2,1)S(1)}, bf16[128,128]{1,0:T(8,128)(2,1)S(1)}, u32[]{:S(2)}, u32[]{:S(2)}) collective-permute-start(bf16[128,128]{1,0:T(8,128)(2,1)S(1)} %join.1), channel_id=1, source_target_pairs={{0,24},{4,28},{8,16},{12,20},{16,8},{20,12},{24,0},{28,4},{1,25},{... | collective-permute-start | bytes 98312 | tf_op jit(solution)/shard_map/ppermute | solution.py:346
  19.3 0.8 %collective-permute-start.3 = (bf16[128,128]{1,0:T(8,128)(2,1)S(1)}, bf16[128,128]{1,0:T(8,128)(2,1)S(1)}, u32[]{:S(2)}, u32[]{:S(2)}) collective-permute-start(bf16[128,128]{1,0:T(8,128)(2,1)S(1)} %join.1), channel_id=1, source_target_pairs={{0,8},{4,12},{8,0},{12,4},{16,24},{20,28},{24,16},{28,20},{1,9},{5... | collective-permute-start | bytes 98312 | tf_op jit(solution)/shard_map/ppermute | solution.py:346
  20.1 1.4 %collective-permute-done.5 = bf16[128,128]{1,0:T(8,128)(2,1)S(1)} collective-permute-done((bf16[128,128]{1,0:T(8,128)(2,1)S(1)}, bf16[128,128]{1,0:T(8,128)(2,1)S(1)}, u32[]{:S(2)}, u32[]{:S(2)}) %collective-permute-start.5) | collective-permute-done | bytes 32800 | tf_op jit(solution)/shard_map/ppermute | solution.py:346
  21.5 2.6 %collective-permute-done.4 = bf16[128,128]{1,0:T(8,128)(2,1)S(1)} collective-permute-done((bf16[128,128]{1,0:T(8,128)(2,1)S(1)}, bf16[128,128]{1,0:T(8,128)(2,1)S(1)}, u32[]{:S(2)}, u32[]{:S(2)}) %collective-permute-start.4) | collective-permute-done | bytes 32800 | tf_op jit(solution)/shard_map/ppermute | solution.py:346
  24.1 0.0 collective-permute-done.3
  24.1 1.6 %collective-permute-start.8 = (bf16[512,128]{1,0:T(8,128)(2,1)S(1)}, bf16[512,128]{1,0:T(8,128)(2,1)S(1)}, u32[]{:S(2)}, u32[]{:S(2)}) collective-permute-start(bf16[512,128]{1,0:T(8,128)(2,1)S(1)} %pad_maximum_fusion.refs_0_), channel_id=1, source_target_pairs={{0,3},{1,2},{2,1},{3,0},{4,7},{5,6},{6,5},{7,4},{8,11},{9,10},{10,... | collective-permute-start | bytes 393224 | tf_op jit(solution)/shard_map/ppermute | solution.py:343
  25.7 0.5 %collective-permute-start.7 = (bf16[512,128]{1,0:T(8,128)(2,1)S(1)}, bf16[512,128]{1,0:T(8,128)(2,1)S(1)}, u32[]{:S(2)}, u32[]{:S(2)}) collective-permute-start(bf16[512,128]{1,0:T(8,128)(2,1)S(1)} %pad_maximum_fusion.refs_0_), channel_id=1, source_target_pairs={{0,2},{1,3},{2,0},{3,1},{4,6},{5,7},{6,4},{7,5},{8,10},{9,11},{10,... | collective-permute-start | bytes 393224 | tf_op jit(solution)/shard_map/ppermute | solution.py:343
  26.2 1.5 %collective-permute-start.6 = (bf16[512,128]{1,0:T(8,128)(2,1)S(1)}, bf16[512,128]{1,0:T(8,128)(2,1)S(1)}, u32[]{:S(2)}, u32[]{:S(2)}) collective-permute-start(bf16[512,128]{1,0:T(8,128)(2,1)S(1)} %pad_maximum_fusion.refs_0_), channel_id=1, source_target_pairs={{0,1},{1,0},{2,3},{3,2},{4,5},{5,4},{6,7},{7,6},{8,9},{9,8},{10,11... | collective-permute-start | bytes 393224 | tf_op jit(solution)/shard_map/ppermute | solution.py:343
  27.7 2.5 %collective-permute-done.8.refs_3_ = bf16[512,128]{1,0:T(8,128)(2,1)S(1)} collective-permute-done((bf16[512,128]{1,0:T(8,128)(2,1)S(1)}, bf16[512,128]{1,0:T(8,128)(2,1)S(1)}, u32[]{:S(2)}, u32[]{:S(2)}) %collective-permute-start.8) | collective-permute-done | bytes 131104 | tf_op jit(solution)/shard_map/ppermute | solution.py:343
  30.2 1.3 %collective-permute-done.7.refs_2_ = bf16[512,128]{1,0:T(8,128)(2,1)S(1)} collective-permute-done((bf16[512,128]{1,0:T(8,128)(2,1)S(1)}, bf16[512,128]{1,0:T(8,128)(2,1)S(1)}, u32[]{:S(2)}, u32[]{:S(2)}) %collective-permute-start.7) | collective-permute-done | bytes 131104 | tf_op jit(solution)/shard_map/ppermute | solution.py:343
  31.5 0.1 collective-permute-done.6.refs_1_
  31.6 0.4 %collective-permute-start.10 = (bf16[512,128]{1,0:T(8,128)(2,1)S(1)}, bf16[512,128]{1,0:T(8,128)(2,1)S(1)}, u32[]{:S(2)}, u32[]{:S(2)}) collective-permute-start(bf16[512,128]{1,0:T(8,128)(2,1)S(1)} %collective-permute-done.6.refs_1_), channel_id=1, source_target_pairs={{0,4},{4,0},{8,12},{12,8},{16,20},{20,16},{24,28},{28,24},{1,5},{5... | collective-permute-start | bytes 393224 | tf_op jit(solution)/shard_map/ppermute | solution.py:352
  32.0 0.5 %own_features.1.refs_8_ = f32[16,4096]{1,0:T(8,128)S(1)} custom-call(bf16[512,128]{1,0:T(8,128)(2,1)S(1)} %pad_maximum_fusion.refs_0_, bf16[512,128]{1,0:T(8,128)(2,1)S(1)} %collective-permute-done.6.refs_1_, bf16[512,128]{1,0:T(8,128)(2,1)S(1)} %collective-permute-done.7.refs_2_, bf16[512,128]{1,0:T(8,128)(2,1)S(1)} %collective-permute-done.8.refs_3_), custom_call_target="tpu_custom_call" | custom-call | tf_op jit(solution)/shard_map/own_features/pallas_call | solution.py:323
  32.5 0.0 collective-permute-done.12.refs_7_
  32.6 0.3 collective-permute-done.11.refs_6_
  32.8 0.2 collective-permute-done.10.refs_5_
  33.0 4.0 %gram.1 = (f32[1024,512]{1,0:T(8,128)}, f32[16,4096]{1,0:T(8,128)}) custom-call(bf16[512,128]{1,0:T(8,128)(2,1)S(1)} %pad_maximum_fusion.refs_0_, bf16[512,128]{1,0:T(8,128)(2,1)S(1)} %collective-permute-done.6.refs_1_, bf16[512,128]{1,0:T(8,128)(2,1)S(1)} %collective-permute-done.7.refs_2_, bf16[512,128]{1,0:T(8,128)(2,1)S(1)} %collective-permute-done.8.refs_3_, ...), custom_call_target="tpu_custom_call" | custom-call | tf_op jit(solution)/shard_map/gram/pallas_call | solution.py:275
  (7 shorter events, 0.1 us)
Async XLA Ops:
  7.0 6.1 %collective-permute-start = (bf16[208,128]{1,0:T(8,128)(2,1)S(1)}, bf16[208,128]{1,0:T(8,128)(2,1)S(1)}, u32[]{:S(2)}, u32[]{:S(2)}) collective-permute-start(bf16[208,128]{1,0:T(8,128)(2,1)S(1)} %get-tuple-element.9), channel_id=1, source_target_pairs={{0,3},{1,2},{2,1},{3,0},{4,7},{5,6},{6,5},{7,4},{8,11},{9,10},{10,... | collective-permute-start | bytes 159752 | tf_op jit(solution)/shard_map/ppermute | solution.py:343
  11.0 4.1 %collective-permute-start.1 = (bf16[208,128]{1,0:T(8,128)(2,1)S(1)}, bf16[208,128]{1,0:T(8,128)(2,1)S(1)}, u32[]{:S(2)}, u32[]{:S(2)}) collective-permute-start(bf16[208,128]{1,0:T(8,128)(2,1)S(1)} %get-tuple-element.10), channel_id=1, source_target_pairs={{0,2},{1,3},{2,0},{3,1},{4,6},{5,7},{6,4},{7,5},{8,10},{9,11},{10,... | collective-permute-start | bytes 159752 | tf_op jit(solution)/shard_map/ppermute | solution.py:343
  11.5 4.1 %collective-permute-start.2 = (bf16[208,128]{1,0:T(8,128)(2,1)S(1)}, bf16[208,128]{1,0:T(8,128)(2,1)S(1)}, u32[]{:S(2)}, u32[]{:S(2)}) collective-permute-start(bf16[208,128]{1,0:T(8,128)(2,1)S(1)} %get-tuple-element.11), channel_id=1, source_target_pairs={{0,1},{1,0},{2,3},{3,2},{4,5},{5,4},{6,7},{7,6},{8,9},{9,8},{10,11... | collective-permute-start | bytes 159752 | tf_op jit(solution)/shard_map/ppermute | solution.py:343
  15.6 5.9 %collective-permute-start.5 = (bf16[128,128]{1,0:T(8,128)(2,1)S(1)}, bf16[128,128]{1,0:T(8,128)(2,1)S(1)}, u32[]{:S(2)}, u32[]{:S(2)}) collective-permute-start(bf16[128,128]{1,0:T(8,128)(2,1)S(1)} %join.1), channel_id=1, source_target_pairs={{0,24},{4,28},{8,16},{12,20},{16,8},{20,12},{24,0},{28,4},{1,25},{... | collective-permute-start | bytes 98312 | tf_op jit(solution)/shard_map/ppermute | solution.py:346
  19.3 4.8 %collective-permute-start.4 = (bf16[128,128]{1,0:T(8,128)(2,1)S(1)}, bf16[128,128]{1,0:T(8,128)(2,1)S(1)}, u32[]{:S(2)}, u32[]{:S(2)}) collective-permute-start(bf16[128,128]{1,0:T(8,128)(2,1)S(1)} %join.1), channel_id=1, source_target_pairs={{0,16},{4,20},{8,24},{12,28},{16,0},{20,4},{24,8},{28,12},{1,17},{... | collective-permute-start | bytes 98312 | tf_op jit(solution)/shard_map/ppermute | solution.py:346
  19.3 4.8 %collective-permute-start.3 = (bf16[128,128]{1,0:T(8,128)(2,1)S(1)}, bf16[128,128]{1,0:T(8,128)(2,1)S(1)}, u32[]{:S(2)}, u32[]{:S(2)}) collective-permute-start(bf16[128,128]{1,0:T(8,128)(2,1)S(1)} %join.1), channel_id=1, source_target_pairs={{0,8},{4,12},{8,0},{12,4},{16,24},{20,28},{24,16},{28,20},{1,9},{5... | collective-permute-start | bytes 98312 | tf_op jit(solution)/shard_map/ppermute | solution.py:346
  24.1 6.0 %collective-permute-start.8 = (bf16[512,128]{1,0:T(8,128)(2,1)S(1)}, bf16[512,128]{1,0:T(8,128)(2,1)S(1)}, u32[]{:S(2)}, u32[]{:S(2)}) collective-permute-start(bf16[512,128]{1,0:T(8,128)(2,1)S(1)} %pad_maximum_fusion.refs_0_), channel_id=1, source_target_pairs={{0,3},{1,2},{2,1},{3,0},{4,7},{5,6},{6,5},{7,4},{8,11},{9,10},{10,... | collective-permute-start | bytes 393224 | tf_op jit(solution)/shard_map/ppermute | solution.py:343
  25.7 5.8 %collective-permute-start.7 = (bf16[512,128]{1,0:T(8,128)(2,1)S(1)}, bf16[512,128]{1,0:T(8,128)(2,1)S(1)}, u32[]{:S(2)}, u32[]{:S(2)}) collective-permute-start(bf16[512,128]{1,0:T(8,128)(2,1)S(1)} %pad_maximum_fusion.refs_0_), channel_id=1, source_target_pairs={{0,2},{1,3},{2,0},{3,1},{4,6},{5,7},{6,4},{7,5},{8,10},{9,11},{10,... | collective-permute-start | bytes 393224 | tf_op jit(solution)/shard_map/ppermute | solution.py:343
  26.2 5.4 %collective-permute-start.6 = (bf16[512,128]{1,0:T(8,128)(2,1)S(1)}, bf16[512,128]{1,0:T(8,128)(2,1)S(1)}, u32[]{:S(2)}, u32[]{:S(2)}) collective-permute-start(bf16[512,128]{1,0:T(8,128)(2,1)S(1)} %pad_maximum_fusion.refs_0_), channel_id=1, source_target_pairs={{0,1},{1,0},{2,3},{3,2},{4,5},{5,4},{6,7},{7,6},{8,9},{9,8},{10,11... | collective-permute-start | bytes 393224 | tf_op jit(solution)/shard_map/ppermute | solution.py:343
  27.7 4.8 %collective-permute-start.9 = (bf16[512,128]{1,0:T(8,128)(2,1)S(1)}, bf16[512,128]{1,0:T(8,128)(2,1)S(1)}, u32[]{:S(2)}, u32[]{:S(2)}) collective-permute-start(bf16[512,128]{1,0:T(8,128)(2,1)S(1)} %pad_maximum_fusion.refs_0_), channel_id=1, source_target_pairs={{0,4},{4,0},{8,12},{12,8},{16,20},{20,16},{24,28},{28,24},{1,5},{5... | collective-permute-start | bytes 393224 | tf_op jit(solution)/shard_map/ppermute | solution.py:352
  30.2 2.4 %collective-permute-start.12 = (bf16[512,128]{1,0:T(8,128)(2,1)S(1)}, bf16[512,128]{1,0:T(8,128)(2,1)S(1)}, u32[]{:S(2)}, u32[]{:S(2)}) collective-permute-start(bf16[512,128]{1,0:T(8,128)(2,1)S(1)} %collective-permute-done.8.refs_3_), channel_id=1, source_target_pairs={{0,4},{4,0},{8,12},{12,8},{16,20},{20,16},{24,28},{28,24},{1,5},{5... | collective-permute-start | bytes 393224 | tf_op jit(solution)/shard_map/ppermute | solution.py:352
  31.5 1.3 %collective-permute-start.11 = (bf16[512,128]{1,0:T(8,128)(2,1)S(1)}, bf16[512,128]{1,0:T(8,128)(2,1)S(1)}, u32[]{:S(2)}, u32[]{:S(2)}) collective-permute-start(bf16[512,128]{1,0:T(8,128)(2,1)S(1)} %collective-permute-done.7.refs_2_), channel_id=1, source_target_pairs={{0,4},{4,0},{8,12},{12,8},{16,20},{20,16},{24,28},{28,24},{1,5},{5... | collective-permute-start | bytes 393224 | tf_op jit(solution)/shard_map/ppermute | solution.py:352
  31.6 1.4 %collective-permute-start.10 = (bf16[512,128]{1,0:T(8,128)(2,1)S(1)}, bf16[512,128]{1,0:T(8,128)(2,1)S(1)}, u32[]{:S(2)}, u32[]{:S(2)}) collective-permute-start(bf16[512,128]{1,0:T(8,128)(2,1)S(1)} %collective-permute-done.6.refs_1_), channel_id=1, source_target_pairs={{0,4},{4,0},{8,12},{12,8},{16,20},{20,16},{24,28},{28,24},{1,5},{5... | collective-permute-start | bytes 393224 | tf_op jit(solution)/shard_map/ppermute | solution.py:352
